TPU v7x, 32 devices: a 4x4x1 block of a 4x4x8 slice. The times are simulated.
32 devices in a mesh: dp: 1 (over z), ep: 32 (over y, x, core).
Axes of the slice: x: 4, y: 4, z: 1, core: 2. Of those that a mesh axis runs over, the one named last changes fastest.
The devices are a block of a 4x4x8 slice.
Arguments:
- x_in: bfloat16 [8192, 448], P(('dp', 'ep'))
- d_out: bfloat16 [8192, 448], P(('dp', 'ep'))
- idx_a: int32 [8192, 8], P(('dp', 'ep'))
- gate_a: float32 [8192, 8], P(('dp', 'ep'))
- idx_b: int32 [8192, 8], P(('dp', 'ep'))
- gate_b: float32 [8192, 8], P(('dp', 'ep'))
- w1_a: bfloat16 [64, 448, 320], P('ep')
- w3_a: bfloat16 [64, 448, 320], P('ep')
- w2_a: bfloat16 [64, 320, 448], P('ep')
- ws1_a: bfloat16 [448, 2560], replicated
- ws3_a: bfloat16 [448, 2560], replicated
- ws2_a: bfloat16 [2560, 448], replicated
- w1_b: bfloat16 [64, 448, 320], P('ep')
- w3_b: bfloat16 [64, 448, 320], P('ep')
- w2_b: bfloat16 [64, 320, 448], P('ep')
- ws1_b: bfloat16 [448, 2560], replicated
- ws3_b: bfloat16 [448, 2560], replicated
- ws2_b: bfloat16 [2560, 448], replicated
Outputs:
- output 1: bfloat16 [8192, 448], P(('dp', 'ep'))
- output 2: bfloat16 [8192, 448], P(('dp', 'ep'))
- output 3: float32 [64, 448, 320], P(('dp', 'ep'))
- output 4: float32 [64, 448, 320], P(('dp', 'ep'))
- output 5: float32 [64, 320, 448], P(('dp', 'ep'))
- output 6: float32 [64, 448, 320], P(('dp', 'ep'))
- output 7: float32 [64, 448, 320], P(('dp', 'ep'))
- output 8: float32 [64, 320, 448], P(('dp', 'ep'))
- output 9: float32 [8192, 8], P(('dp', 'ep'))
- output 10: float32 [8192, 8], P(('dp', 'ep'))
All inputs are finite; a program needn't handle non-finite values.
Results may differ from a plain program's by a relative error of at most 0.0116113.
Values are sent between devices in bfloat16 or wider.
A program may use at most 768 MiB of HBM per device.

v0:
```python
import jax
import jax.numpy as jnp
from jax import lax
from jax.sharding import PartitionSpec as P


def slot_capacity(tokens, n_experts, top_k):
    return top_k * ((2 * tokens + n_experts - 1) // n_experts)


def route_tables(expert_ids, n_experts, capacity):
    flat_ids = expert_ids.reshape(-1)
    pair_count = flat_ids.shape[0]
    pair_order = jnp.argsort(flat_ids, stable=True)
    expert_count = jax.ops.segment_sum(jnp.ones_like(flat_ids), flat_ids, num_segments=n_experts)
    expert_start = jnp.cumsum(expert_count) - expert_count
    position = flat_ids * capacity + jnp.argsort(pair_order) - expert_start[flat_ids]
    slot_index = jnp.arange(capacity)
    src_pair = pair_order[jnp.minimum(expert_start[:, None] + slot_index[None, :], pair_count - 1)]
    slot_used = slot_index[None, :] < expert_count[:, None]
    return src_pair.reshape(-1), slot_used.reshape(-1), position


def to_experts(rows, group_size, capacity):
    n_local = rows.shape[0] // (group_size * capacity)
    row_shape = rows.shape[1:]
    shaped = rows.reshape((group_size, n_local, capacity) + row_shape)
    received = lax.all_to_all(shaped, 'ep', 0, 2, tiled=True)
    return received.reshape((n_local, group_size * capacity) + row_shape)


def to_sources(rows, group_size, capacity):
    n_local = rows.shape[0]
    row_shape = rows.shape[2:]
    shaped = rows.reshape((1, n_local, group_size * capacity) + row_shape)
    received = lax.all_to_all(shaped, 'ep', 2, 0, tiled=True)
    return received.reshape((group_size * n_local * capacity,) + row_shape)


def swiglu_grads(pre_gate, pre_up, d_hidden):
    sigma = jax.nn.sigmoid(pre_gate)
    d_gate = d_hidden * pre_up * sigma * (1.0 + pre_gate * (1.0 - sigma))
    d_up = d_hidden * pre_gate * sigma
    return d_gate.astype(jnp.bfloat16), d_up.astype(jnp.bfloat16)


def expert_hidden(rows, w_gate, w_up):
    pre_gate = jnp.einsum('erd,edf->erf', rows, w_gate, preferred_element_type=jnp.float32)
    pre_up = jnp.einsum('erd,edf->erf', rows, w_up, preferred_element_type=jnp.float32)
    return pre_gate, pre_up, (jax.nn.silu(pre_gate) * pre_up).astype(jnp.bfloat16)


def shared_hidden(rows, s_gate, s_up):
    pre_gate = jnp.dot(rows, s_gate, preferred_element_type=jnp.float32)
    pre_up = jnp.dot(rows, s_up, preferred_element_type=jnp.float32)
    return pre_gate, pre_up, (jax.nn.silu(pre_gate) * pre_up).astype(jnp.bfloat16)


def shared_input_grad(x_rows, d_next, s_gate, s_up, s_down):
    pre = shared_hidden(x_rows, s_gate, s_up)
    projected = jnp.einsum('td,fd->tf', d_next, s_down, preferred_element_type=jnp.float32)
    ds_gate, ds_up = swiglu_grads(pre[0], pre[1], projected)
    return (jnp.einsum('tf,df->td', ds_gate, s_gate, preferred_element_type=jnp.float32)
            + jnp.einsum('tf,df->td', ds_up, s_up, preferred_element_type=jnp.float32))


def send_rows(rows, tables, top_k, group_size, capacity):
    sent = jnp.where(tables[1][:, None], rows[tables[0] // top_k], 0)
    return to_experts(sent, group_size, capacity)


def layer_forward(x_rows, tables, gates, weights, group_size, capacity):
    w_gate, w_up, w_down, s_gate, s_up, s_down = weights
    tokens, top_k = gates.shape
    received = send_rows(x_rows, tables, top_k, group_size, capacity)
    hidden = expert_hidden(received, w_gate, w_up)[2]
    expert_out = jnp.einsum('erf,efd->erd', hidden, w_down,
                            preferred_element_type=jnp.float32).astype(jnp.bfloat16)
    returned = to_sources(expert_out, group_size, capacity)
    per_pair = returned[tables[2]].reshape(tokens, top_k, -1)
    shared = jnp.dot(shared_hidden(x_rows, s_gate, s_up)[2], s_down, preferred_element_type=jnp.float32)
    mixed = x_rows.astype(jnp.float32) + shared + jnp.sum(gates[:, :, None] * per_pair, axis=1)
    return mixed.astype(jnp.bfloat16), received


def layer_backward(x_rows, d_next, tables, gates, weights, received, group_size, capacity):
    w_gate, w_up, w_down, s_gate, s_up, s_down = weights
    tokens, top_k = gates.shape
    src_pair, slot_used, position = tables
    dy_rows = to_experts(jnp.where(slot_used[:, None], d_next[src_pair // top_k], 0), group_size, capacity)
    gate_rows = to_experts(jnp.where(slot_used, gates.reshape(-1)[src_pair], 0.0), group_size, capacity)
    pre_gate, pre_up, hidden = expert_hidden(received, w_gate, w_up)
    projected = jnp.einsum('erd,efd->erf', dy_rows, w_down, preferred_element_type=jnp.float32)
    gate_grad = jnp.sum(hidden.astype(jnp.float32) * projected, axis=2)
    scaled = (gate_rows[:, :, None] * dy_rows).astype(jnp.bfloat16)
    dw_down = jnp.einsum('erf,erd->efd', hidden, scaled, preferred_element_type=jnp.float32)
    da_gate, da_up = swiglu_grads(pre_gate, pre_up, gate_rows[:, :, None] * projected)
    dw_gate = jnp.einsum('erd,erf->edf', received, da_gate, preferred_element_type=jnp.float32)
    dw_up = jnp.einsum('erd,erf->edf', received, da_up, preferred_element_type=jnp.float32)
    d_sent = (jnp.einsum('erf,edf->erd', da_gate, w_gate, preferred_element_type=jnp.float32)
              + jnp.einsum('erf,edf->erd', da_up, w_up, preferred_element_type=jnp.float32)
              ).astype(jnp.bfloat16)
    du_back = to_sources(d_sent, group_size, capacity)
    gate_back = to_sources(gate_grad, group_size, capacity)
    du_pair = du_back[position].reshape(tokens, top_k, -1)
    d_gates = gate_back[position].reshape(tokens, top_k)
    shared_dx = shared_input_grad(x_rows, d_next, s_gate, s_up, s_down)
    d_rows = d_next.astype(jnp.float32) + shared_dx + jnp.sum(du_pair, axis=1, dtype=jnp.float32)
    return d_rows.astype(jnp.bfloat16), dw_gate, dw_up, dw_down, d_gates


def solution(mesh):
    group_size = mesh.shape['ep']
    token_spec = P(('dp', 'ep'), None)
    expert_spec = P('ep', None, None)
    shared_spec = P(None, None)
    grad_spec = P(('dp', 'ep'), None, None)
    layer_specs = (expert_spec,) * 3 + (shared_spec,) * 3

    def device_step(x_in, d_out, idx_a, gate_a, idx_b, gate_b,
                    w1_a, w3_a, w2_a, ws1_a, ws3_a, ws2_a,
                    w1_b, w3_b, w2_b, ws1_b, ws3_b, ws2_b):
        weights_a = (w1_a, w3_a, w2_a, ws1_a, ws3_a, ws2_a)
        weights_b = (w1_b, w3_b, w2_b, ws1_b, ws3_b, ws2_b)
        tokens, top_k = idx_a.shape
        n_experts = w1_a.shape[0] * group_size
        capacity = slot_capacity(tokens, n_experts, top_k)
        tables_a = route_tables(idx_a, n_experts, capacity)
        tables_b = route_tables(idx_b, n_experts, capacity)
        x_mid = layer_forward(x_in, tables_a, gate_a, weights_a, group_size, capacity)[0]
        x_last, kept_b = layer_forward(x_mid, tables_b, gate_b, weights_b, group_size, capacity)
        d_mid, dw1_b, dw3_b, dw2_b, dgate_b = layer_backward(
            x_mid, d_out, tables_b, gate_b, weights_b, kept_b, group_size, capacity)
        resent_a = send_rows(x_in, tables_a, top_k, group_size, capacity)
        d_first, dw1_a, dw3_a, dw2_a, dgate_a = layer_backward(
            x_in, d_mid, tables_a, gate_a, weights_a, resent_a, group_size, capacity)
        return (x_last, d_first, dw1_a, dw3_a, dw2_a, dw1_b, dw3_b, dw2_b, dgate_a, dgate_b)

    in_specs = (token_spec,) * 6 + layer_specs + layer_specs
    out_specs = (token_spec, token_spec) + (grad_spec,) * 6 + (token_spec, token_spec)
    return jax.shard_map(device_step, mesh=mesh, in_specs=in_specs, out_specs=out_specs, check_vma=False)
```

profile of v0, /device:TPU:97, one launch (start us, length us, event | category | flops | bytes accessed | tf_op | source)
XLA Modules:
  0.0 845.4 jit_solution(13046492935720155868)
XLA Ops:
  1.8 14.7 %scatter_custom_fusion = s32[64]{0:T(128)S(1)} fusion(s32[2048]{0:T(1024)S(1)} %reshape.896, s32[2048]{0:T(1024)S(1)} %broadcast.633, s32[]{:T(128)} %constant.53.clone.1), kind=kCustom, calls=%fused_computation.236 | custom fusion | flops 2048 | bytes 260 | tf_op jit(solution)/shard_map/scatter-add | solution.py:15
  22.1 23.0 %gather_fusion = s32[4096]{0:T(1024)S(1)} fusion(s32[2048]{0:T(1024)S(1)} %get-tuple-element.14, s32[4096]{0:T(1024)S(1)} %broadcast_clamp_fusion.5), kind=kCustom, calls=%fused_computation | custom fusion | bytes 49152 | tf_op jit(solution)/shard_map/gather | solution.py:19
  45.5 17.3 %gather_fusion.1 = bf16[4096,448]{1,0:T(8,128)(2,1)} fusion(bf16[256,448]{1,0:T(8,128)(2,1)S(1)} %copy.191, s32[4096]{0:T(1024)S(1)} %broadcast_clamp_fusion.1), kind=kCustom, calls=%fused_computation.1 | custom fusion | bytes 7356416 | tf_op jit(solution)/shard_map/gather | solution.py:68
  76.3 15.2 %scatter_custom_fusion.1 = s32[64]{0:T(128)S(1)} fusion(s32[2048]{0:T(1024)S(1)} %reshape.904, s32[2048]{0:T(1024)S(1)} %broadcast.633, s32[]{:T(128)} %constant.53.clone.1), kind=kCustom, calls=%fused_computation.234 | custom fusion | flops 2048 | bytes 260 | tf_op jit(solution)/shard_map/scatter-add | solution.py:15
  103.6 23.0 %gather_fusion.3 = s32[4096]{0:T(1024)S(1)} fusion(s32[2048]{0:T(1024)S(1)} %get-tuple-element.16, s32[4096]{0:T(1024)S(1)} %broadcast_clamp_fusion.4), kind=kCustom, calls=%fused_computation.3 | custom fusion | bytes 49152 | tf_op jit(solution)/shard_map/gather | solution.py:19
  142.0 11.1 %copy.195 = bf16[1,2,2048,448]{3,1,0,2:T(2,128)(2,1)} copy(bf16[1,2,2048,448]{2,3,1,0:T(8,128)(2,1)} %convert_bitcast_fusion.1) | data formatting | bytes 7340032 | tf_op jit(solution)/shard_map/reshape | solution.py:35
  161.0 23.0 %gather_fusion.6 = f32[4096]{0:T(1024)S(1)} fusion(f32[2048]{0:T(1024)S(1)} %reshape.622, s32[4096]{0:T(1024)S(1)} %broadcast_clamp_fusion.3), kind=kCustom, calls=%fused_computation.6 | custom fusion | bytes 49152 | tf_op jit(solution)/shard_map/gather | solution.py:91
  185.0 17.3 %gather_fusion.7 = bf16[4096,448]{1,0:T(8,128)(2,1)} fusion(bf16[256,448]{1,0:T(8,128)(2,1)S(1)} %copy.214, s32[4096]{0:T(1024)S(1)} %broadcast_clamp_fusion), kind=kCustom, calls=%fused_computation.7 | custom fusion | bytes 7356416 | tf_op jit(solution)/shard_map/gather | solution.py:90
  211.0 36.2 %fusion.28 = s32[2048]{0:T(1024)S(1)} fusion(pred[2048]{0:T(1024)(128)(4,1)S(1)} %get-tuple-element.171, pred[2048]{0:T(1024)(128)(4,1)S(1)} %get-tuple-element.170, pred[2048]{0:T(1024)(128)(4,1)S(1)} %get-tuple-element.169, pred[2048]{0:T(1024)(128)(4,1)S(1)} %get-tuple-element.168, pred[2048]{0:T(1024)(128)(4,1)S(1)} %get-tuple-element.167, ...), kind=kLoop, calls=%fused_computation.224 | loop fusion | flops 131072 | bytes 149732 | tf_op jit(solution)/shard_map/gather | solution.py:80
  265.8 12.0 %gather_fusion.2 = bf16[2048,448]{1,0:T(8,128)(2,1)} fusion(bf16[4096,448]{1,0:T(8,128)(2,1)} %bitcast.276, s32[2048]{0:T(1024)S(1)} %fusion.28), kind=kCustom, calls=%fused_computation.2 | custom fusion | bytes 3678208 | tf_op jit(solution)/shard_map/gather | solution.py:80
  286.1 17.4 %gather_fusion.4 = bf16[4096,448]{1,0:T(8,128)(2,1)} fusion(bf16[256,448]{1,0:T(8,128)(2,1)S(1)} %copy.203, s32[4096]{0:T(1024)S(1)} %broadcast_clamp_fusion), kind=kCustom, calls=%fused_computation.4 | custom fusion | bytes 7356416 | tf_op jit(solution)/shard_map/gather | solution.py:68
  309.4 59.1 %all_to_all.185 = bf16[32,2,64,448]{3,2,1,0:T(8,128)(2,1)} all-to-all(bf16[32,2,64,448]{3,2,1,0:T(8,128)(2,1)} %get-tuple-element.187), channel_id=1, replica_groups=mesh['dp'=1,'ep'=32] {'ep'}, dimensions={0} | all-to-all | bytes 7340032 | tf_op jit(solution)/shard_map/all_to_all | solution.py:28
  374.4 23.0 %gather_fusion.9 = f32[4096]{0:T(1024)S(1)} fusion(f32[2048]{0:T(1024)S(1)} %reshape.626, s32[4096]{0:T(1024)S(1)} %broadcast_clamp_fusion.2), kind=kCustom, calls=%fused_computation.9 | custom fusion | bytes 49152 | tf_op jit(solution)/shard_map/gather | solution.py:91
  410.1 16.7 %all-to-all-done.5 = bf16[32,2,64,448]{3,2,1,0:T(8,128)(2,1)} async-done(((bf16[32,2,64,448]{3,2,1,0:T(8,128)(2,1)}), bf16[32,2,64,448]{3,2,1,0:T(8,128)(2,1)}, u32[]{:S(2)}, u32[]{:S(2)}) %all-to-all-start.5) | async-done | bytes 3670048 | tf_op jit(solution)/shard_map/all_to_all | solution.py:28
  480.1 11.1 %copy.217 = bf16[1,2,2048,448]{3,1,0,2:T(2,128)(2,1)} copy(bf16[1,2,2048,448]{2,3,1,0:T(8,128)(2,1)} %fusion.6) | data formatting | bytes 7340032 | tf_op jit(solution)/shard_map/reshape | solution.py:35
  512.1 11.1 %copy.207 = bf16[1,2,2048,448]{3,1,0,2:T(2,128)(2,1)} copy(bf16[1,2,2048,448]{2,3,1,0:T(8,128)(2,1)} %convert_bitcast_fusion) | data formatting | bytes 7340032 | tf_op jit(solution)/shard_map/reshape | solution.py:35
  523.3 25.9 %all-to-all-done.6 = bf16[1,2,2048,448]{3,1,0,2:T(2,128)(2,1)} async-done(((bf16[1,2,2048,448]{3,1,0,2:T(2,128)(2,1)}), bf16[1,2,2048,448]{3,1,0,2:T(2,128)(2,1)}, u32[]{:S(2)}, u32[]{:S(2)}) %all-to-all-start.6) | async-done | bytes 3670048 | tf_op jit(solution)/shard_map/all_to_all | solution.py:36
  564.0 36.1 %fusion.29 = s32[2048]{0:T(1024)S(1)} fusion(pred[2048]{0:T(1024)(128)(4,1)S(1)} %get-tuple-element.114, pred[2048]{0:T(1024)(128)(4,1)S(1)} %get-tuple-element.113, pred[2048]{0:T(1024)(128)(4,1)S(1)} %get-tuple-element.112, pred[2048]{0:T(1024)(128)(4,1)S(1)} %get-tuple-element.111, pred[2048]{0:T(1024)(128)(4,1)S(1)} %get-tuple-element.110, ...), kind=kLoop, calls=%fused_computation.225 | loop fusion | flops 131072 | bytes 149732 | tf_op jit(solution)/shard_map/gather | solution.py:80
  630.5 17.3 %gather_fusion.10 = bf16[4096,448]{1,0:T(8,128)(2,1)} fusion(bf16[256,448]{1,0:T(8,128)(2,1)S(1)} %copy.223, s32[4096]{0:T(1024)S(1)} %copy-done.42), kind=kCustom, calls=%fused_computation.10 | custom fusion | bytes 7356416 | tf_op jit(solution)/shard_map/gather | solution.py:90
  674.3 11.8 %gather_fusion.13 = f32[2048]{0:T(1024)S(1)} fusion(f32[4096]{0:T(1024)S(1)} %reshape.634, s32[2048]{0:T(1024)S(1)} %fusion.29), kind=kCustom, calls=%fused_computation.13 | custom fusion | bytes 24576 | tf_op jit(solution)/shard_map/gather | solution.py:106
  752.3 11.1 %copy.226 = bf16[1,2,2048,448]{3,1,0,2:T(2,128)(2,1)} copy(bf16[1,2,2048,448]{2,3,1,0:T(8,128)(2,1)} %fusion.7) | data formatting | bytes 7340032 | tf_op jit(solution)/shard_map/reshape | solution.py:35
  794.4 11.8 %gather_fusion.12 = f32[2048]{0:T(1024)S(1)} fusion(f32[4096]{0:T(1024)S(1)} %reshape.631, s32[2048]{0:T(1024)S(1)} %copy-done.46), kind=kCustom, calls=%fused_computation.12 | custom fusion | bytes 24576 | tf_op jit(solution)/shard_map/gather | solution.py:106
  806.9 14.3 %all-to-all-done.9 = bf16[1,2,2048,448]{3,1,0,2:T(2,128)(2,1)} async-done(((bf16[1,2,2048,448]{3,1,0,2:T(2,128)(2,1)}), bf16[1,2,2048,448]{3,1,0,2:T(2,128)(2,1)}, u32[]{:S(2)}, u32[]{:S(2)}) %all-to-all-start.9) | async-done | bytes 3670048 | tf_op jit(solution)/shard_map/all_to_all | solution.py:36
  826.5 10.6 %gather_fusion.11 = bf16[2048,448]{1,0:T(8,128)(2,1)S(1)} fusion(bf16[4096,448]{1,0:T(8,128)(2,1)} %bitcast.275, s32[2048]{0:T(1024)S(1)} %copy-done.46), kind=kCustom, calls=%fused_computation.11 | custom fusion | bytes 3678208 | tf_op jit(solution)/shard_map/gather | solution.py:105
  (288 shorter events, 372.9 us)
Async XLA Ops:
  0.6 603.0 %copy-start = (bf16[448,2560]{1,0:T(8,128)(2,1)S(1)}, bf16[448,2560]{1,0:T(8,128)(2,1)}, u32[]{:S(2)}) copy-start(bf16[448,2560]{1,0:T(8,128)(2,1)} %param.34) | copy-start | bytes 6881284
  22.1 23.2 %copy-start.30 = (bf16[256,448]{0,1:T(8,128)(2,1)S(1)}, bf16[256,448]{0,1:T(8,128)(2,1)}, u32[]{:S(2)}) copy-start(bf16[256,448]{0,1:T(8,128)(2,1)} %param.18) | copy-start | bytes 688132
  45.2 17.6 %copy-start.41 = (s32[4096]{0:T(1024)}, s32[4096]{0:T(1024)S(1)}, u32[]{:S(2)}) copy-start(s32[4096]{0:T(1024)S(1)} %broadcast_clamp_fusion.1) | copy-start | bytes 49156
  66.7 35.3 %copy-start.50 = (f32[256,8]{0,1:T(8,128)S(1)}, f32[256,8]{0,1:T(8,128)}, u32[]{:S(2)}) copy-start(f32[256,8]{0,1:T(8,128)} %param.21) | copy-start | bytes 24580
  66.7 36.6 %copy-start.51 = (f32[256,8]{0,1:T(8,128)S(1)}, f32[256,8]{0,1:T(8,128)}, u32[]{:S(2)}) copy-start(f32[256,8]{0,1:T(8,128)} %param.23) | copy-start | bytes 24580
  66.7 61.4 %all-to-all-start = ((bf16[32,2,64,448]{3,2,1,0:T(8,128)(2,1)}), bf16[32,2,64,448]{3,2,1,0:T(8,128)(2,1)}, u32[]{:S(2)}, u32[]{:S(2)}) async-start(bf16[32,2,64,448]{3,2,1,0:T(8,128)(2,1)} %broadcast_select_fusion.3), calls=%async_computation | async-start | bytes 8388608 | tf_op jit(solution)/shard_map/all_to_all | solution.py:28
  103.5 23.2 %copy-start.34 = (f32[256,8]{1,0:T(8,128)}, f32[256,8]{1,0:T(8,128)S(1)}, u32[]{:S(2)}) copy-start(f32[256,8]{1,0:T(8,128)S(1)} %copy.200) | copy-start | bytes 24580
  153.1 100.5 %all-to-all-start.1 = ((bf16[1,2,2048,448]{3,1,0,2:T(2,128)(2,1)}), bf16[1,2,2048,448]{3,1,0,2:T(2,128)(2,1)}, u32[]{:S(2)}, u32[]{:S(2)}) async-start(bf16[1,2,2048,448]{3,1,0,2:T(2,128)(2,1)} %copy.195), calls=%async_computation.1 | async-start | bytes 8388608 | tf_op jit(solution)/shard_map/all_to_all | solution.py:36
  211.0 40.3 %copy-start.27 = (bf16[448,2560]{1,0:T(8,128)(2,1)S(1)}, bf16[448,2560]{1,0:T(8,128)(2,1)}, u32[]{:S(2)}) copy-start(bf16[448,2560]{1,0:T(8,128)(2,1)} %param.28) | copy-start | bytes 6881284
  247.2 18.6 %copy-start.45 = (s32[2048]{0:T(1024)}, s32[2048]{0:T(1024)S(1)}, u32[]{:S(2)}) copy-start(s32[2048]{0:T(1024)S(1)} %fusion.28) | copy-start | bytes 24580
  253.6 55.8 %all-to-all-start.4 = ((f32[32,1,128]{2,1,0:T(1,128)}), f32[32,1,128]{2,1,0:T(1,128)S(1)}, u32[]{:S(2)}, u32[]{:S(2)}) async-start(f32[32,1,128]{2,1,0:T(1,128)} %reshape.1324), calls=%async_computation.4 | async-start | bytes 32768 | tf_op jit(solution)/shard_map/all_to_all | solution.py:28
  286.0 17.5 %copy-start.31 = (bf16[256,448]{0,1:T(8,128)(2,1)}, bf16[256,448]{0,1:T(8,128)(2,1)S(1)}, u32[]{:S(2)}) copy-start(bf16[256,448]{0,1:T(8,128)(2,1)S(1)} %fusion.26) | copy-start | bytes 688132
  368.5 58.4 %all-to-all-start.5 = ((bf16[32,2,64,448]{3,2,1,0:T(8,128)(2,1)}), bf16[32,2,64,448]{3,2,1,0:T(8,128)(2,1)}, u32[]{:S(2)}, u32[]{:S(2)}) async-start(bf16[32,2,64,448]{3,2,1,0:T(8,128)(2,1)} %get-tuple-element.188), calls=%async_computation.5 | async-start | bytes 8388608 | tf_op jit(solution)/shard_map/all_to_all | solution.py:28
  426.8 38.9 %all-to-all-start.7 = ((f32[32,1,128]{2,1,0:T(1,128)}), f32[32,1,128]{2,1,0:T(1,128)S(1)}, u32[]{:S(2)}, u32[]{:S(2)}) async-start(f32[32,1,128]{2,1,0:T(1,128)} %reshape.1326), calls=%async_computation.7 | async-start | bytes 32768 | tf_op jit(solution)/shard_map/all_to_all | solution.py:28
  465.7 25.5 %all-to-all-start.11 = ((f32[32,1,128]{2,1,0:T(1,128)}), f32[32,1,128]{2,1,0:T(1,128)S(1)}, u32[]{:S(2)}, u32[]{:S(2)}) async-start(f32[32,1,128]{2,1,0:T(1,128)} %reshape.1330), calls=%async_computation.11 | async-start | bytes 32768 | tf_op jit(solution)/shard_map/all_to_all | solution.py:36
  491.2 58.0 %all-to-all-start.6 = ((bf16[1,2,2048,448]{3,1,0,2:T(2,128)(2,1)}), bf16[1,2,2048,448]{3,1,0,2:T(2,128)(2,1)}, u32[]{:S(2)}, u32[]{:S(2)}) async-start(bf16[1,2,2048,448]{3,1,0,2:T(2,128)(2,1)} %copy.217), calls=%async_computation.6 | async-start | bytes 8388608 | tf_op jit(solution)/shard_map/all_to_all | solution.py:36
  523.3 76.9 %copy-start.36 = (bf16[256,448]{0,1:T(8,128)(2,1)S(1)}, bf16[256,448]{0,1:T(8,128)(2,1)}, u32[]{:S(2)}) copy-start(bf16[256,448]{0,1:T(8,128)(2,1)} %param.19) | copy-start | bytes 688132
  549.2 102.6 %all-to-all-start.3 = ((bf16[1,2,2048,448]{3,1,0,2:T(2,128)(2,1)}), bf16[1,2,2048,448]{3,1,0,2:T(2,128)(2,1)}, u32[]{:S(2)}, u32[]{:S(2)}) async-start(bf16[1,2,2048,448]{3,1,0,2:T(2,128)(2,1)} %copy.207), calls=%async_computation.3 | async-start | bytes 8388608 | tf_op jit(solution)/shard_map/all_to_all | solution.py:36
  564.0 38.7 %copy-start.26 = (bf16[448,2560]{1,0:T(8,128)(2,1)S(1)}, bf16[448,2560]{1,0:T(8,128)(2,1)}, u32[]{:S(2)}) copy-start(bf16[448,2560]{1,0:T(8,128)(2,1)} %param.33) | copy-start | bytes 6881284
  564.0 38.7 %copy-start.32 = (bf16[256,448]{0,1:T(8,128)(2,1)S(1)}, bf16[256,448]{0,1:T(8,128)(2,1)}, u32[]{:S(2)}) copy-start(bf16[256,448]{0,1:T(8,128)(2,1)} %copy-done.31) | copy-start | bytes 688132
  651.8 57.7 %all-to-all-start.8 = ((bf16[32,2,64,448]{3,2,1,0:T(8,128)(2,1)}), bf16[32,2,64,448]{3,2,1,0:T(8,128)(2,1)}, u32[]{:S(2)}, u32[]{:S(2)}) async-start(bf16[32,2,64,448]{3,2,1,0:T(8,128)(2,1)} %broadcast_select_fusion.2), calls=%async_computation.8 | async-start | bytes 8388608 | tf_op jit(solution)/shard_map/all_to_all | solution.py:28
  659.5 52.7 %copy-start.47 = (f32[2,2048]{1,0:T(2,128)}, f32[2,2048]{1,0:T(2,128)S(1)}, u32[]{:S(2)}) copy-start(f32[2,2048]{1,0:T(2,128)S(1)} %mul.201) | copy-start | bytes 49156
  735.0 28.4 %all-to-all-start.10 = ((f32[32,1,128]{2,1,0:T(1,128)}), f32[32,1,128]{2,1,0:T(1,128)S(1)}, u32[]{:S(2)}, u32[]{:S(2)}) async-start(f32[32,1,128]{2,1,0:T(1,128)} %reshape.1328), calls=%async_computation.10 | async-start | bytes 32768 | tf_op jit(solution)/shard_map/all_to_all | solution.py:36
  763.4 57.8 %all-to-all-start.9 = ((bf16[1,2,2048,448]{3,1,0,2:T(2,128)(2,1)}), bf16[1,2,2048,448]{3,1,0,2:T(2,128)(2,1)}, u32[]{:S(2)}, u32[]{:S(2)}) async-start(bf16[1,2,2048,448]{3,1,0,2:T(2,128)(2,1)} %copy.226), calls=%async_computation.9 | async-start | bytes 8388608 | tf_op jit(solution)/shard_map/all_to_all | solution.py:36
  (47 other events, 238.3 us)
where the time goes:
time: 858 us; the launch traced here: 845 us
  local copies, waits for them, and re-layouts  341 us (40%)
  other arithmetic  179 us (21%)
  matrix products  115 us (13%)
  starting transfers between devices  83.2 us (10%)
  waiting for transfers between devices  65.4 us (8%)
  blocking collectives  59.1 us (7%)
    gather x2, other arithmetic, layer_forward(): per_pair = returned[tables[2]].reshape(tokens, top_k, -1)  72.3 us
    all_to_all x1, blocking collectives, to_experts(): received = lax.all_to_all(shaped, 'ep', 0, 2, tiled=True)  59.1 us
    all_to_all x6, starting transfers between devices, to_sources(): received = lax.all_to_all(shaped, 'ep', 2, 0, tiled=True)  46.3 us
    gather x4, local copies, waits for them, and re-layouts, layer_backward(): gates.reshape(-1)[src_pair]  46.2 us
    gather x2, local copies, waits for them, and re-layouts, route_tables(): pair_order[jnp.minimum(expert_start[:, None] + slot_index[None, :], pair_...  46.1 us
    reshape x6, local copies, waits for them, and re-layouts, to_sources(): shaped = rows.reshape((1, n_local, group_size * capacity) + row_shape)  45.7 us
    all_to_all x6, waiting for transfers between devices, to_sources(): received = lax.all_to_all(shaped, 'ep', 2, 0, tiled=True)  40.2 us
    all_to_all x5, starting transfers between devices, to_experts(): received = lax.all_to_all(shaped, 'ep', 0, 2, tiled=True)  36.9 us
  transfers between devices with their start and end apart: 11, of which 5 were waited for; matrix products, arithmetic and copies ran while one was open for 58% of the time, Pallas kernels for 0%

commit v1 on v0

v1 whole, which is shorter than its diff:
```python
import functools
import math

import jax
import jax.numpy as jnp
from jax import lax
from jax.experimental import pallas as pl
from jax.experimental.pallas import tpu as pltpu
from jax.sharding import PartitionSpec as P

MESH = pl.DeviceIdType.MESH
F32, BF16 = jnp.float32, jnp.bfloat16
NT = (((1,), (1,)), ((), ()))
VMEM_LIMIT = 60 * 2 ** 20


def dev(i):
    return {'ep': i}


class Torus:
    def __init__(self, n):
        self.nx = math.isqrt(n // 2)
        self.ny = n // 2 // self.nx
        self.me = lax.axis_index('ep')
        self.c = lax.rem(self.me, 2)
        chip = self.me // 2
        self.x, self.y = lax.rem(chip, self.nx), chip // self.nx

    def at(self, dx, dy, c=None):
        x = lax.rem(self.x + dx + self.nx, self.nx)
        y = lax.rem(self.y + dy + self.ny, self.ny)
        return (y * self.nx + x) * 2 + (self.c if c is None else c)


def barrier_all(n):
    me = lax.axis_index('ep')
    b = pltpu.get_barrier_semaphore()

    def body(k, _):
        pl.semaphore_signal(b, inc=1, device_id=dev(lax.rem(me + k, n)), device_id_type=MESH)
        return 0

    lax.fori_loop(1, n, body, 0)
    pl.semaphore_wait(b, n - 1)


def remote(src, dst, ssem, rsem, to):
    return pltpu.make_async_remote_copy(src_ref=src, dst_ref=dst, send_sem=ssem, recv_sem=rsem,
                                        device_id=dev(to), device_id_type=MESH)


class Gather:
    def __init__(self, torus, out, ssem, rsem, rows):
        self.t, self.out, self.ssem, self.rsem = torus, out, ssem, rsem
        self.half, self.quarter = rows // 2, rows // 4
        self.count, self.sent, self.sibling, self.m = 0, [], [], {}

    def ref(self, off, r0, nr, core=None):
        return self.out.at[self.t.at(off[0], off[1], core), pl.ds(r0, nr), :]

    def move(self, off, r0, nr, to):
        i = self.count
        self.count += 1
        ref = self.ref(off, r0, nr)
        cp = remote(ref, ref, self.ssem.at[i], self.rsem.at[i], self.t.at(*to))
        cp.start()
        self.sent.append(cp)
        return i, nr

    def wait(self, off, r0, mv):
        i, nr = mv
        ref = self.ref(off, r0, nr)
        remote(ref, ref, self.ssem.at[i], self.rsem.at[i], self.t.at(1, 0)).wait_recv()

    def to_sibling(self, off, r0, nr):
        i = self.count
        self.count += 1
        ref = self.ref(off, r0, nr)
        cp = remote(ref, ref, self.ssem.at[i], self.rsem.at[i], self.t.at(0, 0, 1 - self.t.c))
        cp.start()
        self.sent.append(cp)
        self.sibling.append((off, r0, nr, i))

    @staticmethod
    def ax(h, d, e=0):
        return (d, e) if h == 0 else (e, d)

    def start(self):
        ax, m = self.ax, self.m
        for h in (0, 1):
            for d in (1, -1):
                m[h, 1, d] = self.move((0, 0), h * self.half, self.half, ax(h, d))
        for h in (0, 1):
            for d in (1, -1):
                m[h, 2, 0, d] = self.move((0, 0), h * self.half, self.half, ax(h, 0, d))
        self.to_sibling((0, 0), 0, 2 * self.half)

    def run(self):
        ax, m, half, q = self.ax, self.m, self.half, self.quarter
        for h in (0, 1):
            for k, d in enumerate((1, -1)):
                self.wait(ax(h, -d), h * half, m[h, 1, d])
                m[h, 1, d, 'f'] = self.move(ax(h, -d), h * half + k * q, q, ax(h, d))
                for e in (1, -1):
                    m[h, 2, -d, e] = self.move(ax(h, -d), h * half, half, ax(h, 0, e))
                self.to_sibling(ax(h, -d), h * half, half)
        for h in (0, 1):
            for k, e in enumerate((1, -1)):
                self.wait(ax(h, 0, -e), h * half, m[h, 2, 0, e])
                m[h, 2, 0, e, 'f'] = self.move(ax(h, 0, -e), h * half + k * q, q, ax(h, 0, e))
                self.to_sibling(ax(h, 0, -e), h * half, half)
        for h in (0, 1):
            for k, d in enumerate((1, -1)):
                self.wait(ax(h, -2 * d), h * half + k * q, m[h, 1, d, 'f'])
            for e in (1, -1):
                m[h, 2, 2, e] = self.move(ax(h, 2), h * half, half, ax(h, 0, e))
            self.to_sibling(ax(h, 2), h * half, half)
        for b in (-1, 1, 2):
            for h in (0, 1):
                for k, e in enumerate((1, -1)):
                    self.wait(ax(h, b, -e), h * half, m[h, 2, b, e])
                    m[h, 2, b, e, 'f'] = self.move(ax(h, b, -e), h * half + k * q, q, ax(h, 0, e))
                    self.to_sibling(ax(h, b, -e), h * half, half)
        for b in (0, -1, 1, 2):
            for h in (0, 1):
                for k, e in enumerate((1, -1)):
                    self.wait(ax(h, b, -2 * e), h * half + k * q, m[h, 2, b, e, 'f'])
                self.to_sibling(ax(h, b, 2), h * half, half)

    def finish(self):
        for off, r0, nr, i in self.sibling:
            ref = self.ref(off, r0, nr, 1 - self.t.c)
            remote(ref, ref, self.ssem.at[i], self.rsem.at[i], self.t.at(1, 0)).wait_recv()
        for cp in self.sent:
            cp.wait_send()


GATHER_SEMS = 80


def gather_kernel(n, x_ref, out_ref, ssem, rsem, lsem):
    t = Torus(n)
    barrier_all(n)
    own = pltpu.make_async_copy(x_ref, out_ref.at[t.me], lsem.at[0])
    own.start()
    own.wait()
    g = Gather(t, out_ref, ssem, rsem, x_ref.shape[0])
    g.start()
    g.run()
    g.finish()


def all_gather(x, n, cid):
    return pl.pallas_call(
        functools.partial(gather_kernel, n),
        out_shape=jax.ShapeDtypeStruct((n,) + x.shape, x.dtype),
        in_specs=[pl.BlockSpec(memory_space=pl.ANY)],
        out_specs=pl.BlockSpec(memory_space=pl.ANY),
        scratch_shapes=[pltpu.SemaphoreType.DMA((GATHER_SEMS,)), pltpu.SemaphoreType.DMA((GATHER_SEMS,)),
                        pltpu.SemaphoreType.DMA((1,))],
        compiler_params=pltpu.CompilerParams(collective_id=cid, has_side_effects=True),
    )(x)


def exchange_kernel(n, *refs):
    count = (len(refs) - 3) // 2
    ins, outs, (ssem, rsem, lsem) = refs[:count], refs[count:2 * count], refs[2 * count:]
    me = lax.axis_index('ep')
    barrier_all(n)
    own = [pltpu.make_async_copy(a.at[me], b.at[me], lsem.at[i]) for i, (a, b) in enumerate(zip(ins, outs))]
    for cp in own:
        cp.start()

    def sends(k):
        to = lax.rem(me + k, n)
        return [remote(a.at[to], b.at[me], ssem.at[i, k], rsem.at[i, k], to)
                for i, (a, b) in enumerate(zip(ins, outs))]

    def arrivals(k):
        fr = lax.rem(me - k + n, n)
        return [remote(a.at[fr], b.at[fr], ssem.at[i, k], rsem.at[i, k], fr)
                for i, (a, b) in enumerate(zip(ins, outs))]

    def start(k, _):
        for cp in sends(k):
            cp.start()
        return 0

    def wait(k, _):
        for cp in arrivals(k):
            cp.wait_recv()
        for cp in sends(k):
            cp.wait_send()
        return 0

    lax.fori_loop(1, n, start, 0)
    lax.fori_loop(1, n, wait, 0)
    for cp in own:
        cp.wait()


def exchange(arrays, n, cid):
    count = len(arrays)
    return pl.pallas_call(
        functools.partial(exchange_kernel, n),
        out_shape=[jax.ShapeDtypeStruct(a.shape, a.dtype) for a in arrays],
        in_specs=[pl.BlockSpec(memory_space=pl.ANY)] * count,
        out_specs=[pl.BlockSpec(memory_space=pl.ANY)] * count,
        scratch_shapes=[pltpu.SemaphoreType.DMA((count, n)), pltpu.SemaphoreType.DMA((count, n)),
                        pltpu.SemaphoreType.DMA((count,))],
        compiler_params=pltpu.CompilerParams(collective_id=cid, has_side_effects=True),
    )(*arrays)


def mm(a, b):
    return jnp.dot(a, b, preferred_element_type=F32)


def mm_nt(a, b):
    return lax.dot_general(a, b, NT, preferred_element_type=F32)


def slots_of(gates):
    tokens = gates.shape[1]
    before = (lax.broadcasted_iota(jnp.int32, (tokens, tokens), 0)
              < lax.broadcasted_iota(jnp.int32, (tokens, tokens), 1))
    member = gates > 0.0
    count = mm(jnp.where(member, 1.0, 0.0).astype(BF16), jnp.where(before, 1.0, 0.0).astype(BF16))
    return jnp.where(member, count, -1.0)


def pick(slot_rows, capacity):
    tokens = slot_rows[0].shape[1]
    want = lax.broadcasted_iota(jnp.int32, (capacity, tokens), 0).astype(F32)
    return jnp.concatenate([jnp.where(s == want, 1.0, 0.0) for s in slot_rows], axis=0)


def split3(v):
    a = v.astype(BF16).astype(F32)
    r = v - a
    b = r.astype(BF16).astype(F32)
    return a, b, r - b


def swap_halves(first, second):
    low = lax.broadcasted_iota(jnp.int32, first.shape, 1) < first.shape[1] // 2
    return jnp.where(low, first, second), jnp.where(low, second, first)


def hidden_of(a13):
    f = a13.shape[0] // 2
    a1, a3 = a13[:f], a13[f:]
    sigma = jax.nn.sigmoid(a1)
    return a1, a3, sigma, (a1 * sigma * a3).astype(BF16)


def pair_rows(block, p, slots, row, capacity, extra=None):
    out = []
    for s in (2 * p, 2 * p + 1):
        hot = pick([slots[8 * s + row:8 * s + row + 1], slots[8 * s + row + 1:8 * s + row + 2]], capacity).astype(BF16)
        lhs = block[s] if extra is None else jnp.concatenate([block[s], extra[s]], axis=0)
        out.append(mm_nt(lhs, hot))
    return swap_halves(*out)


def forward_kernel(row, capacity, keep, x_ref, g_ref, w13t_ref, w2t_ref, *outs):
    o_ref = outs[0]
    sources = x_ref.shape[0]
    slots = slots_of(g_ref[...].reshape(sources * 8, -1))
    pairs = [pair_rows(x_ref, p, slots, row, capacity) for p in range(sources // 2)]
    o = []
    for e in (0, 1):
        rows = jnp.concatenate([pr[e].astype(BF16) for pr in pairs], axis=1)
        if keep:
            outs[1][e] = rows
        hidden = hidden_of(mm(w13t_ref[e], rows))[3]
        o.append(mm(w2t_ref[e], hidden))
    width = 2 * capacity
    for p in range(sources // 2):
        a, b = swap_halves(o[0][:, p * width:(p + 1) * width], o[1][:, p * width:(p + 1) * width])
        o_ref[2 * p] = a.astype(BF16)
        o_ref[2 * p + 1] = b.astype(BF16)


def backward_kernel(row, capacity, kept, x_ref, dy_ref, g_ref, w13t_ref, w13_ref, w2_ref,
                    dw1_ref, dw3_ref, dw2_ref, du_ref, gg_ref, acc13, acc2):
    sources = dy_ref.shape[0]
    step = pl.program_id(0)

    @pl.when(step == 0)
    def _():
        acc13[...] = jnp.zeros_like(acc13)
        acc2[...] = jnp.zeros_like(acc2)

    d = dy_ref.shape[1]
    width = 2 * capacity
    slots = slots_of(g_ref[...].reshape(sources * 8, -1))
    extra = []
    for s in range(sources):
        parts = split3(g_ref[s])
        extra.append(jnp.concatenate(list(parts) + [jnp.zeros_like(parts[0])], axis=0).astype(BF16))
    if not kept:
        xp = [pair_rows(x_ref, p, slots, row, capacity) for p in range(sources // 2)]
    dyp, gp = [], []
    for p in range(sources // 2):
        raw = []
        for s in (2 * p, 2 * p + 1):
            hot = pick([slots[8 * s + row:8 * s + row + 1], slots[8 * s + row + 1:8 * s + row + 2]],
                       capacity).astype(BF16)
            raw.append(mm_nt(jnp.concatenate([dy_ref[s], extra[s]], axis=0), hot))
        dyp.append(swap_halves(raw[0][:d], raw[1][:d]))
        gates = []
        for r in raw:
            first = r[d + row:d + row + 1] + r[d + 8 + row:d + 9 + row] + r[d + 16 + row:d + 17 + row]
            second = r[d + row + 1:d + row + 2] + r[d + 9 + row:d + 10 + row] + r[d + 17 + row:d + 18 + row]
            low = lax.broadcasted_iota(jnp.int32, first.shape, 1) < capacity
            gates.append(jnp.where(low, first, second))
        gp.append(swap_halves(*gates))
    du, gg = [], []
    for e in (0, 1):
        rows = x_ref[e] if kept else jnp.concatenate([pr[e].astype(BF16) for pr in xp], axis=1)
        dy = jnp.concatenate([pr[e] for pr in dyp], axis=1)
        gate = jnp.concatenate([pr[e] for pr in gp], axis=1)
        a1, a3, sigma, hidden = hidden_of(mm(w13t_ref[e], rows))
        p32 = mm(w2_ref[e], dy.astype(BF16))
        gg.append(jnp.sum(hidden.astype(F32) * p32, axis=0, keepdims=True))
        scaled = (gate * dy).astype(BF16)
        acc2[e] += mm_nt(hidden, scaled)
        q = gate * p32
        da1 = (q * a3 * sigma * (1.0 + a1 * (1.0 - sigma))).astype(BF16)
        da3 = (q * a1 * sigma).astype(BF16)
        da = jnp.concatenate([da1, da3], axis=0)
        acc13[e] += mm_nt(rows, da)
        du.append(mm(w13_ref[e], da))
    for p in range(sources // 2):
        at = slice(p * width, (p + 1) * width)
        for ref, v in ((du_ref, du), (gg_ref, gg)):
            a, b = swap_halves(v[0][:, at], v[1][:, at])
            ref[2 * p] = jnp.broadcast_to(a, ref.shape[1:]).astype(ref.dtype)
            ref[2 * p + 1] = jnp.broadcast_to(b, ref.shape[1:]).astype(ref.dtype)

    @pl.when(step == pl.num_programs(0) - 1)
    def _():
        f = dw1_ref.shape[2]
        for e in (0, 1):
            dw1_ref[e] = acc13[e, :, :f]
            dw3_ref[e] = acc13[e, :, f:]
            dw2_ref[e] = acc2[e]


SOURCES = 4


def whole(a):
    return pl.BlockSpec(a.shape, lambda i: (0,) * a.ndim)


def experts_forward(xg, gr, w13t, w2t, row, capacity, keep):
    n, d, tokens = xg.shape
    lanes = SOURCES * capacity
    out_shape = [jax.ShapeDtypeStruct((n, d, 2 * capacity), BF16)]
    out_specs = [pl.BlockSpec((SOURCES, d, 2 * capacity), lambda i: (i, 0, 0))]
    if keep:
        out_shape.append(jax.ShapeDtypeStruct((2, d, n * capacity), BF16))
        out_specs.append(pl.BlockSpec((2, d, lanes), lambda i: (0, 0, i)))
    return pl.pallas_call(
        functools.partial(forward_kernel, row, capacity, keep),
        grid=(n // SOURCES,),
        out_shape=out_shape, out_specs=out_specs,
        in_specs=[pl.BlockSpec((SOURCES, d, tokens), lambda i: (i, 0, 0)),
                  pl.BlockSpec((SOURCES, 8, tokens), lambda i: (i, 0, 0)), whole(w13t), whole(w2t)],
        compiler_params=pltpu.CompilerParams(vmem_limit_bytes=VMEM_LIMIT),
    )(xg, gr, w13t, w2t)


def experts_backward(x, dyg, gr, w13t, w13, w2, row, capacity, kept):
    n, d, tokens = dyg.shape
    lanes = SOURCES * capacity
    f = w2.shape[1]
    grouped = lambda i: (i, 0, 0)
    x_spec = (pl.BlockSpec((2, d, lanes), lambda i: (0, 0, i)) if kept
              else pl.BlockSpec((SOURCES, d, tokens), grouped))
    grads = [jax.ShapeDtypeStruct((2, d, f), F32)] * 2 + [jax.ShapeDtypeStruct((2, f, d), F32)]
    return pl.pallas_call(
        functools.partial(backward_kernel, row, capacity, kept),
        grid=(n // SOURCES,),
        out_shape=grads + [jax.ShapeDtypeStruct((n, d, 2 * capacity), BF16),
                           jax.ShapeDtypeStruct((n, 8, 2 * capacity), F32)],
        out_specs=[whole(g) for g in grads] + [pl.BlockSpec((SOURCES, d, 2 * capacity), grouped),
                                               pl.BlockSpec((SOURCES, 8, 2 * capacity), grouped)],
        in_specs=[x_spec, pl.BlockSpec((SOURCES, d, tokens), grouped),
                  pl.BlockSpec((SOURCES, 8, tokens), grouped), whole(w13t), whole(w13), whole(w2)],
        scratch_shapes=[pltpu.VMEM((2, d, 2 * f), F32), pltpu.VMEM((2, f, d), F32)],
        compiler_params=pltpu.CompilerParams(vmem_limit_bytes=VMEM_LIMIT),
    )(x, dyg, gr, w13t, w13, w2)


def combine_forward_kernel(row, capacity, o_ref, g_ref, y_ref):
    step = pl.program_id(0)
    senders = o_ref.shape[0]
    slots = slots_of(g_ref[...].reshape(senders * 8, -1))

    @pl.when(step == 0)
    def _():
        y_ref[...] = jnp.zeros_like(y_ref)

    acc = y_ref[...]
    for p in range(senders // 2):
        ks = (2 * p, 2 * p + 1)
        lhs = jnp.concatenate([o_ref[k] for k in ks], axis=1)
        order = [8 * k + row + e for k in ks for e in (0, 1)]
        hot = pick([slots[r:r + 1] for r in order], capacity)
        gates = [g_ref[k, row + e:row + e + 1] for k in ks for e in (0, 1)]
        parts = [split3(g) for g in gates]
        for i in range(3):
            part = jnp.concatenate([jnp.broadcast_to(q[i], (capacity,) + q[i].shape[1:]) for q in parts], axis=0)
            acc = acc + mm(lhs, (hot * part).astype(BF16))
    y_ref[...] = acc


def combine_backward_kernel(row, capacity, du_ref, gg_ref, g_ref, y_ref, dg_ref):
    step = pl.program_id(0)
    senders, d = du_ref.shape[0], du_ref.shape[1]
    slots = slots_of(g_ref[...].reshape(senders * 8, -1))

    @pl.when(step == 0)
    def _():
        y_ref[...] = jnp.zeros_like(y_ref)

    acc = y_ref[...]
    dgs = []
    for p in range(senders // 2):
        ks = (2 * p, 2 * p + 1)
        order = [8 * k + row + e for k in ks for e in (0, 1)]
        hot = pick([slots[r:r + 1] for r in order], capacity).astype(BF16)
        gg = jnp.concatenate([gg_ref[k] for k in ks], axis=1)
        shape = gg.shape
        own = (lax.broadcasted_iota(jnp.int32, shape, 1) // capacity) == lax.broadcasted_iota(jnp.int32, shape, 0)
        parts = split3(jnp.where(own, gg, 0.0))
        small = jnp.concatenate(list(parts) + [jnp.zeros_like(parts[0])], axis=0).astype(BF16)
        lhs = jnp.concatenate([jnp.concatenate([du_ref[k] for k in ks], axis=1), small], axis=0)
        res = mm(lhs, hot)
        acc = acc + res[:d]
        dgs.append((res[d:d + 8] + res[d + 8:d + 16] + res[d + 16:d + 24])[:4])
    y_ref[...] = acc
    dg_ref[...] = jnp.concatenate(dgs, axis=0)


SENDERS = 8


def combine_forward(o, g_own, row, capacity):
    n, d, _ = o.shape
    tokens = g_own.shape[2]
    return pl.pallas_call(
        functools.partial(combine_forward_kernel, row, capacity),
        grid=(n // SENDERS,),
        out_shape=jax.ShapeDtypeStruct((d, tokens), F32),
        out_specs=pl.BlockSpec((d, tokens), lambda i: (0, 0)),
        in_specs=[pl.BlockSpec((SENDERS, d, 2 * capacity), lambda i: (i, 0, 0)),
                  pl.BlockSpec((SENDERS, 8, tokens), lambda i: (i, 0, 0))],
        compiler_params=pltpu.CompilerParams(vmem_limit_bytes=VMEM_LIMIT),
    )(o, g_own)


def combine_backward(du, gg, g_own, row, capacity):
    n, d, _ = du.shape
    tokens = g_own.shape[2]
    return pl.pallas_call(
        functools.partial(combine_backward_kernel, row, capacity),
        grid=(n // SENDERS,),
        out_shape=[jax.ShapeDtypeStruct((d, tokens), F32), jax.ShapeDtypeStruct((2 * n, tokens), F32)],
        out_specs=[pl.BlockSpec((d, tokens), lambda i: (0, 0)),
                   pl.BlockSpec((2 * SENDERS, tokens), lambda i: (i, 0))],
        in_specs=[pl.BlockSpec((SENDERS, d, 2 * capacity), lambda i: (i, 0, 0)),
                  pl.BlockSpec((SENDERS, 8, 2 * capacity), lambda i: (i, 0, 0)),
                  pl.BlockSpec((SENDERS, 8, tokens), lambda i: (i, 0, 0))],
        compiler_params=pltpu.CompilerParams(vmem_limit_bytes=VMEM_LIMIT),
    )(du, gg, g_own)


def swiglu_grads(pre_gate, pre_up, d_hidden):
    sigma = jax.nn.sigmoid(pre_gate)
    d_gate = d_hidden * pre_up * sigma * (1.0 + pre_gate * (1.0 - sigma))
    d_up = d_hidden * pre_gate * sigma
    return d_gate.astype(BF16), d_up.astype(BF16)


def shared_hidden(rows, s_gate, s_up):
    pre_gate, pre_up = mm(rows, s_gate), mm(rows, s_up)
    return pre_gate, pre_up, (jax.nn.silu(pre_gate) * pre_up).astype(BF16)


def shared_input_grad(x_rows, d_next, s_gate, s_up, s_down):
    pre = shared_hidden(x_rows, s_gate, s_up)
    ds_gate, ds_up = swiglu_grads(pre[0], pre[1], mm_nt(d_next, s_down))
    return mm_nt(ds_gate, s_gate) + mm_nt(ds_up, s_up)


def gate_table(idx, gate, n_experts):
    ids = jnp.arange(n_experts, dtype=idx.dtype)[:, None, None]
    return jnp.sum(jnp.where(idx.T[None] == ids, gate.T[None], 0.0), axis=1)


def pair_gates(dg, idx):
    ids = jnp.arange(dg.shape[0], dtype=idx.dtype)[:, None, None]
    return jnp.sum(jnp.where(idx.T[None] == ids, dg[:, None, :], 0.0), axis=0).T


def solution(mesh):
    n = mesh.shape['ep']
    token_spec = P(('dp', 'ep'), None)
    expert_spec = P('ep', None, None)
    shared_spec = P(None, None)
    grad_spec = P(('dp', 'ep'), None, None)
    layer_specs = (expert_spec,) * 3 + (shared_spec,) * 3

    def device_step(x_in, d_out, idx_a, gate_a, idx_b, gate_b,
                    w1_a, w3_a, w2_a, ws1_a, ws3_a, ws2_a,
                    w1_b, w3_b, w2_b, ws1_b, ws3_b, ws2_b):
        tokens, top_k = idx_a.shape
        n_experts = w1_a.shape[0] * n
        capacity = top_k * ((2 * tokens + n_experts - 1) // n_experts)

        def weights(w1, w3, w2):
            w13 = jnp.concatenate([w1, w3], axis=2)
            return jnp.swapaxes(w13, 1, 2), w13, w2, jnp.swapaxes(w2, 1, 2)

        w13t_a, w13_a, w2n_a, w2t_a = weights(w1_a, w3_a, w2_a)
        w13t_b, w13_b, w2n_b, w2t_b = weights(w1_b, w3_b, w2_b)

        odd = lax.rem(lax.axis_index('ep'), 2) == 1
        tables = [gate_table(i, g, n_experts).reshape(n, 2, tokens) for i, g in ((idx_a, gate_a), (idx_b, gate_b))]
        tables = [jnp.where(odd, t[:, ::-1], t) for t in tables]
        g_own = jnp.concatenate(tables + [jnp.zeros((n, 4, tokens), F32)], axis=1)

        (g_recv,) = exchange([g_own], n, 0)
        xg = all_gather(x_in.T, n, 1)
        (o_a,) = experts_forward(xg, g_recv, w13t_a, w2t_a, 0, capacity, False)
        (ret_a,) = exchange([o_a], n, 2)
        mixed_a = combine_forward(ret_a, g_own, 0, capacity)
        shared_a = mm(shared_hidden(x_in, ws1_a, ws3_a)[2], ws2_a)
        x_mid = (x_in.astype(F32) + shared_a + mixed_a.T).astype(BF16)

        x1g = all_gather(x_mid.T, n, 3)
        o_b, rows_b = experts_forward(x1g, g_recv, w13t_b, w2t_b, 2, capacity, True)
        (ret_b,) = exchange([o_b], n, 4)
        mixed_b = combine_forward(ret_b, g_own, 2, capacity)
        shared_b = mm(shared_hidden(x_mid, ws1_b, ws3_b)[2], ws2_b)
        x_last = (x_mid.astype(F32) + shared_b + mixed_b.T).astype(BF16)

        def unswap(dg):
            dg = dg.reshape(n, 2, tokens)
            return jnp.where(odd, dg[:, ::-1], dg).reshape(2 * n, tokens)

        dyg = all_gather(d_out.T, n, 5)
        dw1_b, dw3_b, dw2_b, du_b, gg_b = experts_backward(rows_b, dyg, g_recv, w13t_b, w13_b, w2n_b, 2, capacity, True)
        du_ret_b, gg_ret_b = exchange([du_b, gg_b], n, 6)
        dx_b, dg_b = combine_backward(du_ret_b, gg_ret_b, g_own, 2, capacity)
        shared_dx = shared_input_grad(x_mid, d_out, ws1_b, ws3_b, ws2_b)
        d_mid = (d_out.astype(F32) + shared_dx + dx_b.T).astype(BF16)

        xg2 = all_gather(lax.optimization_barrier((x_in.T, d_mid))[0], n, 7)
        dyg2 = all_gather(d_mid.T, n, 8)
        dw1_a, dw3_a, dw2_a, du_a, gg_a = experts_backward(xg2, dyg2, g_recv, w13t_a, w13_a, w2n_a, 0, capacity, False)
        du_ret_a, gg_ret_a = exchange([du_a, gg_a], n, 9)
        dx_a, dg_a = combine_backward(du_ret_a, gg_ret_a, g_own, 0, capacity)
        shared_dx = shared_input_grad(x_in, d_mid, ws1_a, ws3_a, ws2_a)
        d_first = (d_mid.astype(F32) + shared_dx + dx_a.T).astype(BF16)
        return (x_last, d_first, dw1_a, dw3_a, dw2_a, dw1_b, dw3_b, dw2_b,
                pair_gates(unswap(dg_a), idx_a), pair_gates(unswap(dg_b), idx_b))

    in_specs = (token_spec,) * 6 + layer_specs + layer_specs
    out_specs = (token_spec, token_spec) + (grad_spec,) * 6 + (token_spec, token_spec)
    return jax.shard_map(device_step, mesh=mesh, in_specs=in_specs, out_specs=out_specs, check_vma=False)
```

time: 858 us -> 675 us (0.79)
  Pallas kernels: 0 us -> 583 us
  local copies, waits for them, and re-layouts: 341 us -> 33.1 us
  other arithmetic: 179 us -> 10.4 us
  starting transfers between devices: 83.2 us -> 0 us
  matrix products: 115 us -> 35.9 us
  waiting for transfers between devices: 65.4 us -> 0 us
  blocking collectives: 59.1 us -> 0 us
    pallas_call x0 -> x18, Pallas kernels: none -> 583 us  [the longest x5 269 us: exchange(): pl.pallas_call(functools.partial(exchange_kernel, n), out_shape=[jax.Shap...]
    gather x24 -> x0, local copies, waits for them, and re-layouts: 234 us -> none  [the longest x4 46.2 us: layer_backward(): gates.reshape(-1)[src_pair]]
    gather x12 -> x0, other arithmetic: 83.8 us -> none  [the longest x2 72.3 us: layer_forward(): per_pair = returned[tables[2]].reshape(tokens, top_k, -1)]
    all_to_all x11 -> x0, starting transfers between devices: 83.2 us -> none  [the longest x6 46.3 us: to_sources(): received = lax.all_to_all(shaped, 'ep', 2, 0, tiled=True)]
    dot_general x30 -> x12, matrix products: 115 us -> 35.9 us  [the longest x6 20.3 us: mm(): return jnp.dot(a, b, preferred_element_type=F32)]
    all_to_all x11 -> x0, waiting for transfers between devices: 65.4 us -> none  [the longest x6 40.2 us: to_sources(): received = lax.all_to_all(shaped, 'ep', 2, 0, tiled=True)]
    all_to_all x1 -> x0, blocking collectives: 59.1 us -> none  [to_experts(): received = lax.all_to_all(shaped, 'ep', 0, 2, tiled=True)]
    reshape x12 -> x4, local copies, waits for them, and re-layouts: 46.3 us -> 0.15 us  [the longest x2 0.08 us: device_step(): gate_table(i, g, n_experts).reshape(n, 2, tokens)]
  transfers between devices with their start and end apart: 11 -> 0, of which waited for: 5 -> 0; matrix products, arithmetic and copies ran while one was open for 58% -> 0% of each run, Pallas kernels for 0% -> 0%
where the time goes in v1:
time: 675 us; the launch traced here: 664 us
  Pallas kernels  583 us (86%)
  matrix products  35.9 us (5%)
  local copies, waits for them, and re-layouts  33.1 us (5%)
  other arithmetic  10.4 us (2%)
    pallas_call x5, Pallas kernels, exchange(): pl.pallas_call(functools.partial(exchange_kernel, n), out_shape=[jax.Shap...  269 us
    pallas_call x5, Pallas kernels, all_gather(): pl.pallas_call(functools.partial(gather_kernel, n), out_shape=jax.ShapeDt...  200 us
    pallas_call x2, Pallas kernels, experts_backward(): pl.pallas_call(functools.partial(backward_kernel, row, capacity, kept), g...  53.5 us
    pallas_call x2, Pallas kernels, experts_forward(): pl.pallas_call(functools.partial(forward_kernel, row, capacity, keep), gr...  37.2 us
    unnamed x76, local copies, waits for them, and re-layouts  27.1 us
    dot_general x6, matrix products, mm(): return jnp.dot(a, b, preferred_element_type=F32)  20.3 us
    dot_general x6, matrix products, mm_nt(): return lax.dot_general(a, b, NT, preferred_element_type=F32)  15.6 us

profile of v1, /device:TPU:97, one launch (start us, length us, event | category | flops | bytes accessed | tf_op | source)
XLA Modules:
  0.0 664.2 jit_solution(13574530310231568702)
XLA Ops:
  0.7 4.3 fusion.27
  7.4 40.9 %shard_map.249.x_ref = bf16[32,448,256]{2,1,0:T(8,128)(2,1)} custom-call(bf16[448,256]{1,0:T(8,128)(2,1)} %bitcast.54), custom_call_target="tpu_custom_call" | custom-call | tf_op jit(solution)/shard_map/pallas_call | solution.py:155
  50.2 10.0 %shard_map.250.g_ref = f32[32,8,256]{2,1,0:T(8,128)} custom-call(f32[32,8,256]{2,1,0:T(8,128)} %maximum_maximum_fusion.refs_0_.g_ref), custom_call_target="tpu_custom_call" | custom-call | tf_op jit(solution)/shard_map/pallas_call | solution.py:205
  70.9 18.5 %shard_map.251.refs_0_ = bf16[32,448,128]{2,1,0:T(8,128)(2,1)} custom-call(bf16[32,448,256]{2,1,0:T(8,128)(2,1)} %shard_map.249.x_ref, f32[32,8,256]{2,1,0:T(8,128)} %shard_map.250.g_ref, bf16[2,640,448]{2,1,0:T(8,128)(2,1)} %copy.45.w13t_ref, bf16[2,448,320]{2,1,0:T(8,128)(2,1)} %bitcast.57), custom_call_target="tpu_custom_call" | custom-call | tf_op jit(solution)/shard_map/pallas_call | solution.py:367
  89.5 64.1 %shard_map.252.o_ref = bf16[32,448,128]{2,1,0:T(8,128)(2,1)} custom-call(bf16[32,448,128]{2,1,0:T(8,128)(2,1)} %shard_map.251.refs_0_), custom_call_target="tpu_custom_call" | custom-call | tf_op jit(solution)/shard_map/pallas_call | solution.py:205
  153.6 6.6 shard_map.253
  160.2 4.4 fusion.18
  169.5 39.9 %shard_map.254.x_ref = bf16[32,448,256]{2,1,0:T(8,128)(2,1)} custom-call(bf16[448,256]{1,0:T(8,128)(2,1)} %bitcast.58), custom_call_target="tpu_custom_call" | custom-call | tf_op jit(solution)/shard_map/pallas_call | solution.py:155
  221.0 18.7 %shard_map.255 = (bf16[32,448,128]{2,1,0:T(8,128)(2,1)}, bf16[2,448,2048]{2,1,0:T(8,128)(2,1)}) custom-call(bf16[32,448,256]{2,1,0:T(8,128)(2,1)} %shard_map.254.x_ref, f32[32,8,256]{2,1,0:T(8,128)} %shard_map.250.g_ref, bf16[2,640,448]{2,1,0:T(8,128)(2,1)} %copy.49.w13t_ref, bf16[2,448,320]{2,1,0:T(8,128)(2,1)} %bitcast.56), custom_call_target="tpu_custom_call" | custom-call | tf_op jit(solution)/shard_map/pallas_call | solution.py:367
  239.7 63.2 %shard_map.256.o_ref = bf16[32,448,128]{2,1,0:T(8,128)(2,1)} custom-call(bf16[32,448,128]{2,1,0:T(8,128)(2,1)} %get-tuple-element.31.refs_0_), custom_call_target="tpu_custom_call" | custom-call | tf_op jit(solution)/shard_map/pallas_call | solution.py:205
  302.9 6.6 shard_map.257
  309.5 4.4 fusion.19
  318.1 41.3 %shard_map.258.dy_ref = bf16[32,448,256]{2,1,0:T(8,128)(2,1)} custom-call(bf16[448,256]{1,0:T(8,128)(2,1)} %bitcast.59), custom_call_target="tpu_custom_call" | custom-call | tf_op jit(solution)/shard_map/pallas_call | solution.py:155
  360.8 25.7 %shard_map.259 = (f32[2,448,320]{2,1,0:T(8,128)}, f32[2,448,320]{2,1,0:T(8,128)}, f32[2,320,448]{2,1,0:T(8,128)}, bf16[32,448,128]{2,1,0:T(8,128)(2,1)}, f32[32,8,128]{2,1,0:T(8,128)}) custom-call(bf16[2,448,2048]{2,1,0:T(8,128)(2,1)} %get-tuple-element.32.x_ref, bf16[32,448,256]{2,1,0:T(8,128)(2,1)} %shard_map.258.dy_ref, f32[32,8,256]{2,1,0:T(8,128)} %shard_map.250.g_ref, ...), custom_call_target="tpu_custom_call" | custom-call | tf_op jit(solution)/shard_map/pallas_call | solution.py:385
  386.5 65.4 %shard_map.260 = (bf16[32,448,128]{2,1,0:T(8,128)(2,1)}, f32[32,8,128]{2,1,0:T(8,128)}) custom-call(bf16[32,448,128]{2,1,0:T(8,128)(2,1)} %get-tuple-element.33.refs_0_, f32[32,8,128]{2,1,0:T(8,128)} %get-tuple-element.34.refs_1_), custom_call_target="tpu_custom_call" | custom-call | tf_op jit(solution)/shard_map/pallas_call | solution.py:205
  451.9 5.5 shard_map.261
  457.4 5.0 fusion.17
  467.6 41.2 %shard_map.262.x_ref = bf16[32,448,256]{2,1,0:T(8,128)(2,1)} custom-call(bf16[448,256]{1,0:T(8,128)(2,1)} %bitcast.55), custom_call_target="tpu_custom_call" | custom-call | tf_op jit(solution)/shard_map/pallas_call | solution.py:155
  508.8 36.5 %shard_map.263.dy_ref = bf16[32,448,256]{2,1,0:T(8,128)(2,1)} custom-call(bf16[448,256]{1,0:T(8,128)(2,1)} %bitcast.60), custom_call_target="tpu_custom_call" | custom-call | tf_op jit(solution)/shard_map/pallas_call | solution.py:155
  546.7 27.8 %shard_map.264 = (f32[2,448,320]{2,1,0:T(8,128)}, f32[2,448,320]{2,1,0:T(8,128)}, f32[2,320,448]{2,1,0:T(8,128)}, bf16[32,448,128]{2,1,0:T(8,128)(2,1)}, f32[32,8,128]{2,1,0:T(8,128)}) custom-call(bf16[32,448,256]{2,1,0:T(8,128)(2,1)} %shard_map.262.x_ref, bf16[32,448,256]{2,1,0:T(8,128)(2,1)} %shard_map.263.dy_ref, f32[32,8,256]{2,1,0:T(8,128)} %shard_map.250.g_ref, ...), custom_call_target="tpu_custom_call" | custom-call | tf_op jit(solution)/shard_map/pallas_call | solution.py:385
  574.5 65.9 %shard_map.265 = (bf16[32,448,128]{2,1,0:T(8,128)(2,1)}, f32[32,8,128]{2,1,0:T(8,128)}) custom-call(bf16[32,448,128]{2,1,0:T(8,128)(2,1)} %get-tuple-element.39.refs_0_, f32[32,8,128]{2,1,0:T(8,128)} %get-tuple-element.40.refs_1_), custom_call_target="tpu_custom_call" | custom-call | tf_op jit(solution)/shard_map/pallas_call | solution.py:205
  640.4 5.5 shard_map.266
  646.0 5.4 fusion.16
  655.8 3.0 copy.54
  (108 shorter events, 53.1 us)
Async XLA Ops:
  0.6 308.9 %copy-start = (bf16[2560,448]{0,1:T(8,128)(2,1)S(1)}, bf16[2560,448]{0,1:T(8,128)(2,1)}, u32[]{:S(2)}) copy-start(bf16[2560,448]{0,1:T(8,128)(2,1)} %param.35) | copy-start | bytes 6881284
  0.7 4.3 copy-start.5
  7.4 40.9 %copy-start.29 = (s32[256,8]{0,1:T(8,128)S(1)}, s32[256,8]{0,1:T(8,128)}, u32[]{:S(2)}) copy-start(s32[256,8]{0,1:T(8,128)} %param.22) | copy-start | bytes 24580
  7.4 40.9 %copy-start.30 = (f32[256,8]{0,1:T(8,128)S(1)}, f32[256,8]{0,1:T(8,128)}, u32[]{:S(2)}) copy-start(f32[256,8]{0,1:T(8,128)} %param.23) | copy-start | bytes 24580
  7.4 41.4 %copy-start.28 = (s32[256,8]{0,1:T(8,128)S(1)}, s32[256,8]{0,1:T(8,128)}, u32[]{:S(2)}) copy-start(s32[256,8]{0,1:T(8,128)} %param.20) | copy-start | bytes 24580
  7.4 41.4 %copy-start.31 = (f32[256,8]{0,1:T(8,128)S(1)}, f32[256,8]{0,1:T(8,128)}, u32[]{:S(2)}) copy-start(f32[256,8]{0,1:T(8,128)} %param.21) | copy-start | bytes 24580
  153.6 6.6 copy-start.6
  160.2 4.4 copy-start.11
  164.6 4.9 copy-start.19
  302.9 6.6 copy-start.20
  309.5 4.4 copy-start.22
  318.1 41.3 %copy-start.3 = (bf16[2,448,320]{2,1,0:T(8,128)(2,1)S(1)}, bf16[2,448,320]{2,1,0:T(8,128)(2,1)}, u32[]{:S(2)}) copy-start(bf16[2,448,320]{2,1,0:T(8,128)(2,1)} %copy.47) | copy-start | bytes 1720324
  318.1 41.3 %copy-start.4 = (bf16[2,448,320]{2,1,0:T(8,128)(2,1)S(1)}, bf16[2,448,320]{2,1,0:T(8,128)(2,1)}, u32[]{:S(2)}) copy-start(bf16[2,448,320]{2,1,0:T(8,128)(2,1)} %copy.46) | copy-start | bytes 1720324
  451.9 5.5 copy-start.14
  451.9 5.5 copy-start.23
  457.4 5.0 copy-start.15
  462.4 5.3 copy-start.24
  508.8 36.5 %copy-start.2 = (bf16[2,448,320]{2,1,0:T(8,128)(2,1)S(1)}, bf16[2,448,320]{2,1,0:T(8,128)(2,1)}, u32[]{:S(2)}) copy-start(bf16[2,448,320]{2,1,0:T(8,128)(2,1)} %copy.42) | copy-start | bytes 1720324
  640.4 5.5 copy-start.18
  640.4 5.5 copy-start.25
  640.4 5.5 copy-start.32
  655.8 5.9 copy-start.26
  655.8 6.1 copy-start.27
  655.8 7.9 %copy-start.1 = (bf16[2560,448]{0,1:T(8,128)(2,1)S(1)}, bf16[2560,448]{0,1:T(8,128)(2,1)}, u32[]{:S(2)}) copy-start(bf16[2560,448]{0,1:T(8,128)(2,1)} %param.35) | copy-start | bytes 6881284
  (9 other events, 23.0 us)

commit v2 on v0

v2 whole, which is shorter than its diff:
```python
import functools
import math
from types import SimpleNamespace

import jax
import jax.numpy as jnp
from jax import lax
from jax.experimental import pallas as pl
from jax.experimental.pallas import tpu as pltpu
from jax.sharding import PartitionSpec as P

MESH = pl.DeviceIdType.MESH
F32, BF16 = jnp.float32, jnp.bfloat16
NT = (((1,), (1,)), ((), ()))
VMEM_LIMIT = 62914560
PAIR = (0, 1)
SIDES = (1, -1)


def dev(i):
    return {'ep': i}


class Torus:
    def __init__(self, n):
        self.nx = math.isqrt(n // 2)
        self.ny = n // 2 // self.nx
        self.me = lax.axis_index('ep')
        self.c = lax.rem(self.me, 2)
        chip = self.me // 2
        self.x, self.y = lax.rem(chip, self.nx), chip // self.nx

    def at(self, dx, dy, c=None):
        x = lax.rem(self.x + dx + self.nx, self.nx)
        y = lax.rem(self.y + dy + self.ny, self.ny)
        return (y * self.nx + x) * 2 + (self.c if c is None else c)


def barrier_all(n):
    me = lax.axis_index('ep')
    b = pltpu.get_barrier_semaphore()

    def body(k, _):
        pl.semaphore_signal(b, inc=1, device_id=dev(lax.rem(me + k, n)), device_id_type=MESH)
        return 0

    lax.fori_loop(1, n, body, 0)
    pl.semaphore_wait(b, n - 1)


def remote(src, dst, ssem, rsem, to):
    return pltpu.make_async_remote_copy(src_ref=src, dst_ref=dst, send_sem=ssem, recv_sem=rsem,
                                        device_id=dev(to), device_id_type=MESH)


def barrier_some(partners):
    b = pltpu.get_barrier_semaphore()
    for p in partners:
        pl.semaphore_signal(b, inc=1, device_id=dev(p), device_id_type=MESH)
    pl.semaphore_wait(b, len(partners))


def around(t, cores):
    steps = [hops(h, d) for h in PAIR for d in SIDES]
    return [t.at(*o, c) for o in steps for c in cores] + [t.at(0, 0, 1 - t.c)]


def run_kernel(body, cid, ins, outs, scratch):
    names = [*ins, *outs, *scratch]

    def kernel(*refs):
        body(SimpleNamespace(**dict(zip(names, refs))))

    spec = lambda space: pl.BlockSpec(memory_space=space)
    res = pl.pallas_call(
        kernel,
        out_shape=[jax.ShapeDtypeStruct(shape, dtype) for shape, dtype, _ in outs.values()],
        in_specs=[spec(space) for _, space in ins.values()],
        out_specs=[spec(space) for _, _, space in outs.values()],
        scratch_shapes=list(scratch.values()),
        compiler_params=pltpu.CompilerParams(collective_id=cid, has_side_effects=True, vmem_limit_bytes=VMEM_LIMIT),
    )(*[array for array, _ in ins.values()])
    return SimpleNamespace(**dict(zip(outs, res)))


RING = 4
HBM, VMEM = pl.ANY, pltpu.VMEM
dma = pltpu.SemaphoreType.DMA


def hops(h, d, e=0):
    return (d, e) if h == 0 else (e, d)


class Gather:
    def __init__(self, torus, r, rows):
        self.t, self.block, self.out, self.ssem, self.rsem, self.lsem = torus, r.block, r.gathered, r.gs, r.gr, r.gl
        self.half, self.quarter = rows // 2, rows // 4
        self.count, self.sent, self.sibling, self.m = 0, [], [], {}

    def ref(self, off, r0, nr, core=None):
        return self.out.at[self.t.at(*off, core), pl.ds(r0, nr), :]

    def send(self, off, r0, nr, to):
        i = self.count
        self.count += 1
        ref = self.ref(off, r0, nr)
        src = self.block.at[pl.ds(r0, nr), :] if off == (0, 0) else ref
        cp = remote(src, ref, self.ssem.at[i], self.rsem.at[i], to)
        cp.start()
        self.sent.append(cp)
        return i

    def move(self, off, r0, nr, to):
        return self.send(off, r0, nr, self.t.at(*to)), nr

    def arrive(self, ref, i):
        remote(ref, ref, self.ssem.at[i], self.rsem.at[i], self.t.at(1, 0)).wait_recv()

    def wait(self, off, r0, mv):
        self.arrive(self.ref(off, r0, mv[1]), mv[0])

    def to_sibling(self, off, r0, nr):
        self.sibling.append((off, r0, nr, self.send(off, r0, nr, self.t.at(0, 0, 1 - self.t.c))))

    def start(self):
        m, half = self.m, self.half
        for h in PAIR:
            for d in SIDES:
                m[h, 'own', d] = self.move((0, 0), h * half, half, hops(h, d))
        for h in PAIR:
            for d in SIDES:
                m[h, 0, d] = self.move((0, 0), h * half, half, hops(h, 0, d))
        self.to_sibling((0, 0), 0, half * 2)
        self.own = pltpu.make_async_copy(self.block, self.out.at[self.t.me], self.lsem.at[0])
        self.own.start()

    def across(self, h, b):
        for k, e in enumerate(SIDES):
            off = hops(h, b, -e)
            self.wait(off, h * self.half, self.m[h, b, e])
            self.m[h, b, e, 'on'] = self.move(off, h * self.half + k * self.quarter, self.quarter, hops(h, 0, e))
            self.to_sibling(off, h * self.half, self.half)

    def spread(self, h, b):
        for e in SIDES:
            self.m[h, b, e] = self.move(hops(h, b), h * self.half, self.half, hops(h, 0, e))
        self.to_sibling(hops(h, b), h * self.half, self.half)

    def run(self, work=None):
        m, half, q = self.m, self.half, self.quarter
        for h in PAIR:
            for k, d in enumerate(SIDES):
                self.wait(hops(h, -d), h * half, m[h, 'own', d])
                m[h, 'on', d] = self.move(hops(h, -d), h * half + k * q, q, hops(h, d))
                self.spread(h, -d)
        for h in PAIR:
            self.across(h, 0)
        for h in PAIR:
            for k, d in enumerate(SIDES):
                self.wait(hops(h, -2 * d), h * half + k * q, m[h, 'on', d])
            self.spread(h, 2)
        if work:
            work()
        for b in (-1, 1, 2):
            for h in PAIR:
                self.across(h, b)
        for b in (0, -1, 1, 2):
            for h in PAIR:
                for k, e in enumerate(SIDES):
                    self.wait(hops(h, b, -2 * e), h * half + k * q, m[h, b, e, 'on'])
                self.to_sibling(hops(h, b, 2), h * half, half)

    def finish(self):
        for off, r0, nr, i in self.sibling:
            self.arrive(self.ref(off, r0, nr, 1 - self.t.c), i)
        for cp in self.sent:
            cp.wait_send()
        self.own.wait()


def gather_parts(block, n):
    sems = dma((80,))
    return ({'block': (block, HBM)}, {'gathered': ((n,) + block.shape, block.dtype, HBM)},
            {'gs': sems, 'gr': sems, 'gl': dma((1,))})


class Exchange:
    def __init__(self, t, n, src, dst, sems):
        self.t, self.n, self.src, self.dst = t, n, src, dst
        self.ss, self.rs, self.ls = sems

    def send(self, k):
        to = lax.rem(self.t.me + k, self.n)
        return remote(self.src(to), self.dst.at[self.t.me], self.ss.at[k], self.rs.at[k], to)

    def start(self):
        def body(k, _):
            self.send(k).start()
            return 0

        self.own = pltpu.make_async_copy(self.src(self.t.me), self.dst.at[self.t.me], self.ls.at[0])
        self.own.start()
        lax.fori_loop(1, self.n, body, 0)

    def finish(self):
        def body(k, _):
            fr = lax.rem(self.t.me - k + self.n, self.n)
            remote(self.src(fr), self.dst.at[fr], self.ss.at[k], self.rs.at[k], fr).wait_recv()
            self.send(k).wait_send()
            return 0

        lax.fori_loop(1, self.n, body, 0)
        self.own.wait()


class Tables:
    def __init__(self, t, n, r):
        self.t, self.r = t, r
        flat = lambda i: r.g.at[i // (2 * t.nx), lax.rem(i // 2, t.nx), lax.rem(i, 2)]
        self.experts = Exchange(t, n, flat, r.g_recv, (r.ts, r.tr, r.tl))

    def start(self):
        t, r = self.t, self.r
        self.own = [pltpu.make_async_copy(r.g.at[t.y], r.by_x.at[t.y], r.tl.at[1]),
                    pltpu.make_async_copy(r.g.at[:, t.x], r.by_y.at[t.x], r.tl.at[2])]
        for cp in self.own:
            cp.start()
        self.lines = []
        for d in range(1, RING):
            y, x = lax.rem(t.y + d, RING), lax.rem(t.x + d, RING)
            fy, fx = lax.rem(t.y + RING - d, RING), lax.rem(t.x + RING - d, RING)
            for h, src, dst, me, fr in ((1, r.g.at[y], r.by_x, t.y, fy), (0, r.g.at[:, x], r.by_y, t.x, fx)):
                self.lines += [remote(src, dst.at[i], r.us.at[h, d], r.ur.at[h, d], t.at(*hops(h, d))) for i in (me, fr)]
        for cp in self.lines[::2]:
            cp.start()
        self.experts.start()

    def finish(self):
        self.experts.finish()
        for cp, arrival in zip(self.lines[::2], self.lines[1::2]):
            arrival.wait_recv()
            cp.wait_send()
        for cp in self.own:
            cp.wait()


CHUNK = 512


class Shared:
    def __init__(self, r):
        self.r = r
        self.copies = [pltpu.make_async_copy(a, b, r.wl.at[i])
                       for i, (a, b) in enumerate(((r.ws1, r.v1), (r.ws3, r.v3), (r.ws2, r.v2)))]
        for cp in self.copies:
            cp.start()

    def ready(self):
        for cp in self.copies:
            cp.wait()

    def loop(self, out, step):
        out[...] = jnp.zeros_like(out)

        def body(i, _):
            out[...] += step(pl.ds(pl.multiple_of(i * CHUNK, CHUNK), CHUNK))
            return 0

        lax.fori_loop(0, self.r.v1.shape[1] // CHUNK, body, 0)

    def forward(self, x_t, out):
        r, x = self.r, x_t.T

        def step(at):
            return mm_nt(r.v2[:, at], hidden_of(mm(x, r.v1[:, at]), mm(x, r.v3[:, at]))[1])

        self.loop(out, step)

    def backward(self, x_t, dy_t, out):
        r, x, dy = self.r, x_t.T, dy_t.T

        def step(at):
            a1, a3 = mm(x, r.v1[:, at]), mm(x, r.v3[:, at])
            da1, da3 = swiglu_grads(a1, a3, mm(dy, r.v2[:, at]))
            return mm_nt(r.v1[:, at], da1) + mm_nt(r.v3[:, at], da3)

        self.loop(out, step)


def shared_parts(ws1, ws3, ws2):
    buf = VMEM(ws1.shape, BF16)
    return ({'ws1': (ws1, HBM), 'ws3': (ws3, HBM), 'ws2': (ws2.T, HBM)},
            {'v1': buf, 'v3': buf, 'v2': buf, 'wl': dma((3,))})


def gather_first(x_t, g, weights, n, cid):
    tokens = g.shape[2]
    side = math.isqrt(n // 2)
    line = ((side, side, 2, 8, tokens), F32, HBM)
    ins, outs, scratch = gather_parts(x_t, n)
    w_ins, w_scratch = shared_parts(*weights)
    table, lines = dma((n,)), dma((2, RING))

    def body(r):
        t = Torus(n)
        shared = Shared(r)
        barrier_all(n)
        gather, tables = Gather(t, r, x_t.shape[0]), Tables(t, n, r)
        gather.start()
        tables.start()
        shared.ready()
        shared.forward(r.x[...], r.s)
        gather.run()
        tables.finish()
        gather.finish()

    res = run_kernel(body, cid, {**ins, **w_ins, 'g': (g.reshape(line[0]), HBM), 'x': (x_t, VMEM)},
                     {**outs, 'g_recv': ((n, 8, tokens), F32, HBM), 'by_x': line, 'by_y': line,
                      's': (x_t.shape, F32, VMEM)},
                     {**scratch, **w_scratch, 'ts': table, 'tr': table, 'tl': dma((3,)), 'us': lines, 'ur': lines})
    return res.gathered, res.g_recv, [a.reshape(side, 2 * side, 8, tokens) for a in (res.by_x, res.by_y)], res.s


def gather_second(block, weights, n, cid):
    ins, outs, scratch = gather_parts(block, n)
    w_ins, w_scratch = shared_parts(*weights)
    d = block.shape[0] // 2
    part = ((d, block.shape[1]), F32, VMEM)

    def body(r):
        t = Torus(n)
        shared = Shared(r)
        barrier_some(around(t, [t.c]))
        gather = Gather(t, r, block.shape[0])
        gather.start()
        shared.ready()
        shared.forward(r.x[:d], r.s)
        gather.run(lambda: shared.backward(r.x[:d], r.x[d:], r.ds))
        gather.finish()

    res = run_kernel(body, cid, {**ins, **w_ins, 'x': (block, VMEM)}, {**outs, 's': part, 'ds': part},
                     {**scratch, **w_scratch})
    return res.gathered, res.s, res.ds


def gather_third(block, n, cid):
    ins, outs, scratch = gather_parts(block, n)

    def body(r):
        t = Torus(n)
        barrier_some(around(t, [t.c]))
        gather = Gather(t, r, block.shape[0])
        gather.start()
        gather.run()
        gather.finish()

    return run_kernel(body, cid, ins, outs, scratch).gathered


def mm(a, b):
    return jnp.dot(a, b, preferred_element_type=F32)


def mm_nt(a, b):
    return lax.dot_general(a, b, NT, preferred_element_type=F32)


def slots_of(gates):
    tokens = gates.shape[1]
    before = (lax.broadcasted_iota(jnp.int32, (tokens, tokens), 0)
              < lax.broadcasted_iota(jnp.int32, (tokens, tokens), 1))
    member = gates > 0.0
    count = mm(jnp.where(member, 1.0, 0.0).astype(BF16), jnp.where(before, 1.0, 0.0).astype(BF16))
    return jnp.where(member, count, -1.0)


def pick(slot_rows, capacity):
    tokens = slot_rows[0].shape[1]
    want = lax.broadcasted_iota(jnp.int32, (capacity, tokens), 0).astype(F32)
    return jnp.concatenate([jnp.where(s == want, 1.0, 0.0) for s in slot_rows], axis=0)


def split3(v):
    a = v.astype(BF16).astype(F32)
    r = v - a
    b = r.astype(BF16).astype(F32)
    return a, b, r - b


def swap_halves(first, second):
    low = lax.broadcasted_iota(jnp.int32, first.shape, 1) < first.shape[1] // 2
    return jnp.where(low, first, second), jnp.where(low, second, first)


def hidden_of(a1, a3):
    sigma = jax.nn.sigmoid(a1)
    return sigma, (a1 * sigma * a3).astype(BF16)


def source_hot(slots, s, row, capacity):
    return pick([slots[8 * s + row:8 * s + row + 1], slots[8 * s + row + 1:8 * s + row + 2]], capacity).astype(BF16)


def pair_rows(block, p, slots, row, capacity):
    return swap_halves(*[mm_nt(block[s], source_hot(slots, s, row, capacity)) for s in (2 * p, 2 * p + 1)])


def forward_kernel(row, capacity, keep, x_ref, g_ref, w1_ref, w3_ref, w2_ref, *outs):
    o_ref, w2t = outs[0], outs[-1]
    sources = x_ref.shape[0]

    @pl.when(pl.program_id(0) == 0)
    def _():
        for e in PAIR:
            w2t[e] = w2_ref[e].T

    slots = slots_of(g_ref[...].reshape(sources * 8, -1))
    pairs = [pair_rows(x_ref, p, slots, row, capacity) for p in range(sources // 2)]
    o = []
    for e in PAIR:
        rows = jnp.concatenate([pr[e].astype(BF16) for pr in pairs], axis=1)
        if keep:
            outs[1][e] = rows
        hidden = hidden_of(mm(w1_ref[e], rows), mm(w3_ref[e], rows))[1]
        o.append(mm(w2t[e], hidden))
    width = 2 * capacity
    for p in range(sources // 2):
        a, b = swap_halves(o[0][:, p * width:(p + 1) * width], o[1][:, p * width:(p + 1) * width])
        o_ref[2 * p] = a.astype(BF16)
        o_ref[2 * p + 1] = b.astype(BF16)


def backward_kernel(row, capacity, kept, x_ref, dy_ref, g_ref, w1_ref, w3_ref, w2_ref,
                    dw1_ref, dw3_ref, dw2_ref, du_ref, gg_ref, w1n, w3n):
    sources = dy_ref.shape[0]

    @pl.when(pl.program_id(0) == 0)
    def _():
        for ref in (dw1_ref, dw3_ref, dw2_ref):
            ref[...] = jnp.zeros_like(ref)
        for e in PAIR:
            w1n[e] = w1_ref[e].T
            w3n[e] = w3_ref[e].T

    d, tokens = dy_ref.shape[1:]
    width = 2 * capacity
    slots = slots_of(g_ref[...].reshape(sources * 8, -1))
    low = lax.broadcasted_iota(jnp.int32, (1, width), 1) < capacity
    if not kept:
        xp = [pair_rows(x_ref, p, slots, row, capacity) for p in range(sources // 2)]
    hots, dyp, gp = [], [], []
    for p in range(sources // 2):
        raw, gates = [], []
        for s in (2 * p, 2 * p + 1):
            hot = source_hot(slots, s, row, capacity)
            hots.append(hot)
            parts = split3(g_ref[s])
            extra = jnp.concatenate(list(parts) + [jnp.zeros_like(parts[0])], axis=0).astype(BF16)
            r = mm_nt(jnp.concatenate([dy_ref[s], extra], axis=0), hot)
            raw.append(r[:d])
            both = [r[d + i:d + i + 1] + r[d + 8 + i:d + 9 + i] + r[d + 16 + i:d + 17 + i] for i in (row, row + 1)]
            gates.append(jnp.where(low, *both))
        dyp.append(swap_halves(*raw))
        gp.append(swap_halves(*gates))
    du, gg = [], []
    for e in PAIR:
        rows = x_ref[e] if kept else jnp.concatenate([pr[e].astype(BF16) for pr in xp], axis=1)
        dy = jnp.concatenate([pr[e] for pr in dyp], axis=1)
        gate = jnp.concatenate([pr[e] for pr in gp], axis=1)
        a1, a3 = mm(w1_ref[e], rows), mm(w3_ref[e], rows)
        sigma, hidden = hidden_of(a1, a3)
        p32 = mm(w2_ref[e], dy.astype(BF16))
        gg.append(jnp.sum(hidden.astype(F32) * p32, axis=0, keepdims=True))
        dw2_ref[e] += mm_nt(hidden, (gate * dy).astype(BF16))
        q = gate * p32
        da1 = (q * a3 * sigma * (1.0 + a1 * (1.0 - sigma))).astype(BF16)
        da3 = (q * a1 * sigma).astype(BF16)
        dw1_ref[e] += mm_nt(da1, rows)
        dw3_ref[e] += mm_nt(da3, rows)
        du.append(mm(w1n[e], da1) + mm(w3n[e], da3))
    for p in range(sources // 2):
        at = slice(p * width, (p + 1) * width)
        for s, v in zip((2 * p, 2 * p + 1), swap_halves(du[0][:, at], du[1][:, at])):
            du_ref[s] = v.astype(BF16)
        for s, v in zip((2 * p, 2 * p + 1), swap_halves(gg[0][:, at], gg[1][:, at])):
            wide = jnp.broadcast_to(v, (8, width))
            own = (lax.broadcasted_iota(jnp.int32, (8, width), 1) // capacity
                   == lax.broadcasted_iota(jnp.int32, (8, width), 0))
            parts = split3(jnp.where(own, wide, 0.0))
            res = mm(jnp.concatenate(list(parts) + [jnp.zeros_like(parts[0])], axis=0).astype(BF16), hots[s])
            gg_ref[s] = (res[:8] + res[8:16] + res[16:24])[:gg_ref.shape[1]]


SOURCES = 4


def whole(a):
    return pl.BlockSpec(a.shape, lambda i: (0,) * a.ndim)


def experts_forward(xg, gr, w1, w3, w2, row, capacity, keep):
    n, d, tokens = xg.shape[0], w1.shape[2], xg.shape[2]
    lanes = SOURCES * capacity
    out_shape = [jax.ShapeDtypeStruct((n, d, 2 * capacity), BF16)]
    out_specs = [pl.BlockSpec((SOURCES, d, 2 * capacity), lambda i: (i, 0, 0))]
    if keep:
        out_shape.append(jax.ShapeDtypeStruct((2, d, n * capacity), BF16))
        out_specs.append(pl.BlockSpec((2, d, lanes), lambda i: (0, 0, i)))
    return pl.pallas_call(
        functools.partial(forward_kernel, row, capacity, keep),
        grid=(n // SOURCES,),
        out_shape=out_shape, out_specs=out_specs,
        in_specs=[pl.BlockSpec((SOURCES, d, tokens), lambda i: (i, 0, 0)),
                  pl.BlockSpec((SOURCES, 8, tokens), lambda i: (i, 0, 0)), whole(w1), whole(w3), whole(w2)],
        scratch_shapes=[pltpu.VMEM((2, d, w2.shape[1]), BF16)],
        compiler_params=pltpu.CompilerParams(vmem_limit_bytes=VMEM_LIMIT),
    )(xg, gr, w1, w3, w2)


def experts_backward(x, dyg, gr, w1, w3, w2, row, capacity, kept):
    n, d, tokens = dyg.shape[0], w1.shape[2], dyg.shape[2]
    lanes = SOURCES * capacity
    f = w2.shape[1]
    grouped = lambda i: (i, 0, 0)
    x_spec = (pl.BlockSpec((2, d, lanes), lambda i: (0, 0, i)) if kept
              else pl.BlockSpec((SOURCES, d, tokens), grouped))
    grads = [jax.ShapeDtypeStruct((2, f, d), F32)] * 3
    return pl.pallas_call(
        functools.partial(backward_kernel, row, capacity, kept),
        grid=(n // SOURCES,),
        out_shape=grads + [jax.ShapeDtypeStruct((n, d, 2 * capacity), BF16),
                           jax.ShapeDtypeStruct((n, 2, tokens), F32)],
        out_specs=[whole(g) for g in grads] + [pl.BlockSpec((SOURCES, d, 2 * capacity), grouped),
                                               pl.BlockSpec((SOURCES, 2, tokens), grouped)],
        in_specs=[x_spec, pl.BlockSpec((SOURCES, d, tokens), lambda i: (i, 1, 0)),
                  pl.BlockSpec((SOURCES, 8, tokens), grouped), whole(w1), whole(w3), whole(w2)],
        scratch_shapes=[pltpu.VMEM((2, d, f), BF16), pltpu.VMEM((2, d, f), BF16)],
        compiler_params=pltpu.CompilerParams(vmem_limit_bytes=VMEM_LIMIT),
    )(x, dyg, gr, w1, w3, w2)


FAR_TO_NEAR = (2, 1, -1, 0)
ROUND_SEMS = 8


class Return:
    def __init__(self, torus, r, name, row, capacity, gated):
        self.t, self.row, self.capacity, self.gated = torus, row, capacity, gated
        for field in ('src', 'out', *RETURN_SCRATCH):
            setattr(self, field, getattr(r, name + field))
        self.tables = (r.by_x, r.by_y)
        self.half = self.src.shape[3] // 2
        self.quarter = self.half // 2
        self.sent = []

    def pos(self, h):
        return (self.t.x, self.t.y) if h == 0 else (self.t.y, self.t.x)

    def source(self, h, p, q, cores):
        rows = pl.ds(h * self.half, self.half)
        a, b = (q, p) if h == 0 else (p, q)
        return self.src.at[a, b, cores, rows, :]

    def push(self, src, dst, h, j, slot, to, second=False):
        ss, rs = (self.ss2, self.rs2) if second else (self.ss, self.rs)
        at = (h, slot) if second else (h, j, slot)
        cp = remote(src, dst, ss.at[at], rs.at[at], to)
        cp.start()
        self.sent.append(cp)

    def arrive(self, dst, h, j, slot, second=False):
        ss, rs = (self.ss2, self.rs2) if second else (self.ss, self.rs)
        at = (h, slot) if second else (h, j, slot)
        remote(dst, dst, ss.at[at], rs.at[at], self.t.at(1, 0)).wait_recv()

    def turn(self, j):
        return 1 if j % 2 == 0 else -1

    def sends(self, j):
        c = self.t.c
        for h in PAIR:
            p, q0 = self.pos(h)
            q = lax.rem(q0 + FAR_TO_NEAR[j] + RING, RING)
            d = self.turn(j)
            self.push(self.source(h, lax.rem(p + 2, RING), q, slice(None)), self.relay.at[h, j], h, j, 0,
                      self.t.at(*hops(h, d)))
            k = p * 2 + c
            for i, d in enumerate(SIDES):
                for core in PAIR:
                    self.direct(h, j, i, d, core, p, q, k)
            self.push(self.source(h, p, q, 1 - c), self.recv.at[h, j, k], h, j, 5, self.t.at(0, 0, 1 - c))
            pltpu.make_async_copy(self.source(h, p, q, c), self.recv.at[h, j, k], self.ls.at[h, j]).start()

    def direct(self, h, j, i, d, core, p, q, k):
        cp = remote(self.source(h, lax.rem(p + d + RING, RING), q, core), self.recv.at[h, j, k],
                    self.ss.at[h, j, 1 + i * 2 + core], self.rs.at[h, j, 1 + i * 2 + self.t.c],
                    self.t.at(*hops(h, d), core))
        cp.start()
        self.sent.append(cp)

    def forward(self, j):
        c, d = self.t.c, self.turn(j)
        for h in PAIR:
            p, _ = self.pos(h)
            self.arrive(self.relay.at[h, j], h, j, 0)
            k = lax.rem(p - d + RING, RING) * 2 + c
            for core in PAIR:
                cp = remote(self.relay.at[h, j, core], self.recv.at[h, j, k], self.ss.at[h, j, 6 + core],
                            self.rs.at[h, j, 6 + c], self.t.at(*hops(h, d), core))
                cp.start()
                self.sent.append(cp)

    def arrivals(self, j):
        for h in PAIR:
            p, q0 = self.pos(h)
            for slot in (1, 2, 3, 4, 5, 6, 7):
                self.arrive(self.recv.at[h, j, 0], h, j, slot)
            q = lax.rem(q0 + FAR_TO_NEAR[j] + RING, RING)
            pltpu.make_async_copy(self.source(h, p, q, self.t.c), self.recv.at[h, j, 0], self.ls.at[h, j]).wait()

    def combine(self, h, j):
        _, q0 = self.pos(h)
        q = lax.rem(q0 + FAR_TO_NEAR[j] + RING, RING)
        gates = self.tables[h][q]
        senders, _, tokens = gates.shape
        slots = slots_of(gates.reshape(senders * 8, tokens))
        acc = None
        for m in range(senders // 2):
            ks = (2 * m, 2 * m + 1)
            lhs = jnp.concatenate([self.recv[h, j, k] for k in ks], axis=1)
            order = [8 * k + self.row + e for k in ks for e in PAIR]
            hot = pick([slots[r:r + 1] for r in order], self.capacity)
            if self.gated:
                parts = [split3(gates[k, self.row + e:self.row + e + 1]) for k in ks for e in PAIR]
                weights = [hot * jnp.concatenate([jnp.broadcast_to(g[i], (self.capacity, tokens)) for g in parts], axis=0)
                           for i in range(3)]
            else:
                weights = [hot]
            for w in weights:
                term = mm(lhs, w.astype(BF16))
                acc = term if acc is None else acc + term
        return acc

    def round(self, j):
        half, quarter = self.half, self.quarter
        for h in PAIR:
            acc = self.combine(h, j)
            up, down = self.t.at(*hops(h, 0, 1)), self.t.at(*hops(h, 0, -1))
            mine = self.part.at[h, j]
            if j == 0:
                self.part[h, j] = acc
                self.push(mine.at[pl.ds(0, quarter)], self.rin.at[h, 0], h, j, 0, up, True)
                self.push(mine.at[pl.ds(quarter, quarter)], self.rin.at[h, 1], h, j, 1, down, True)
            elif j == 1:
                self.arrive(self.rin.at[h, 0], h, j, 0, True)
                self.part[h, j, :quarter] = acc[:quarter] + self.rin[h, 0]
                self.part[h, j, quarter:] = acc[quarter:]
                self.push(mine, self.fin.at[h, 0], h, j, 2, up, True)
            elif j == 2:
                self.arrive(self.rin.at[h, 1], h, j, 1, True)
                self.part[h, j, :quarter] = acc[:quarter]
                self.part[h, j, quarter:] = acc[quarter:] + self.rin[h, 1]
                self.push(mine, self.fin.at[h, 1], h, j, 3, down, True)
            else:
                self.out[h * half:(h + 1) * half, :] = acc

    def finish(self):
        for h in PAIR:
            for i in PAIR:
                self.arrive(self.fin.at[h, i], h, 0, 2 + i, True)
            at = slice(h * self.half, (h + 1) * self.half)
            self.out[at, :] = self.out[at, :] + self.fin[h, 0] + self.fin[h, 1]
        for cp in self.sent:
            cp.wait_send()


RETURN_SCRATCH = ('recv', 'relay', 'part', 'rin', 'fin', 'ss', 'rs', 'ss2', 'rs2', 'ls')


def return_parts(name, rows, tokens, n):
    d, width = rows.shape[1:]
    side = math.isqrt(n // 2)
    half = d // 2
    first, second = dma((2, RING, ROUND_SEMS)), dma((2, RING))
    shapes = (VMEM((2, RING, 2 * RING, half, width), BF16), VMEM((2, RING, 2, half, width), BF16),
              VMEM((2, RING, half, tokens), F32), VMEM((2, 2, half // 2, tokens), F32),
              VMEM((2, 2, half, tokens), F32), first, first, second, second, second)
    return ({name + 'src': (rows.reshape(side, side, 2, d, width), HBM)},
            {**{name + f: shape for f, shape in zip(RETURN_SCRATCH, shapes)}, name + 'out': VMEM((d, tokens), F32)})


def drive(todo, work=None):
    steps = [(r, j) for r in todo for j in range(RING)]
    for r, j in steps[:2]:
        r.sends(j)
    todo[0].forward(0)
    if work:
        work()
    for u, (r, j) in enumerate(steps):
        for later, k in steps[u + 2:u + 3]:
            later.sends(k)
        for later, k in steps[u + 1:u + 2]:
            later.forward(k)
        r.arrivals(j)
        r.round(j)
    for r in todo:
        r.finish()


def gg_parts(gg, n):
    sems = dma((n,))
    return {'gg': (gg, HBM)}, {'dg': (gg.shape, F32, HBM)}, {'qs': sems, 'qr': sems, 'ql': dma((1,))}


def return_first(o, lines, x_t, s, dy_t, row, capacity, n, cid):
    d, tokens = x_t.shape
    ins, scratch = return_parts('o', o, tokens, n)

    def body(r):
        t = Torus(n)
        barrier_some(around(t, PAIR))
        job = Return(t, r, 'o', row, capacity, True)
        drive([job])
        r.block[:d] = (r.x[...].astype(F32) + r.s[...] + job.out[...]).astype(BF16)
        r.block[d:] = r.dy[...]

    return run_kernel(body, cid, {**ins, 'by_x': (lines[0], VMEM), 'by_y': (lines[1], VMEM), 'x': (x_t, VMEM),
                                  's': (s, VMEM), 'dy': (dy_t, VMEM)},
                      {'block': ((2 * d, tokens), BF16, VMEM)}, scratch).block


def return_second(du, o, gg, lines, block, s, ds, x_t, row, capacity, n, cid):
    d, tokens = x_t.shape
    u_ins, u_scratch = return_parts('u', du, tokens, n)
    o_ins, o_scratch = return_parts('o', o, tokens, n)
    g_ins, g_outs, g_scratch = gg_parts(gg, n)

    def body(r):
        t = Torus(n)
        barrier_all(n)
        back = Exchange(t, n, lambda i: r.gg.at[i], r.dg, (r.qs, r.qr, r.ql))
        back.start()
        u, o = Return(t, r, 'u', row, capacity, False), Return(t, r, 'o', row, capacity, True)
        drive([u, o])
        r.last[...] = (r.x1dy[:d].astype(F32) + r.s[...] + o.out[...]).astype(BF16)
        r.block[:d] = r.x[...]
        r.block[d:] = (r.x1dy[d:].astype(F32) + r.ds[...] + u.out[...]).astype(BF16)
        back.finish()

    res = run_kernel(body, cid, {**u_ins, **o_ins, **g_ins, 'by_x': (lines[0], VMEM), 'by_y': (lines[1], VMEM),
                                 'x1dy': (block, VMEM), 's': (s, VMEM), 'ds': (ds, VMEM), 'x': (x_t, VMEM)},
                     {**g_outs, 'last': (x_t.shape, BF16, VMEM), 'block': (block.shape, BF16, VMEM)},
                     {**u_scratch, **o_scratch, **g_scratch})
    return res.last, res.block, res.dg


def return_third(du, gg, lines, block, weights, row, capacity, n, cid):
    d, tokens = block.shape[0] // 2, block.shape[1]
    ins, scratch = return_parts('u', du, tokens, n)
    g_ins, g_outs, g_scratch = gg_parts(gg, n)
    w_ins, w_scratch = shared_parts(*weights)

    def body(r):
        t = Torus(n)
        shared = Shared(r)
        barrier_all(n)
        back = Exchange(t, n, lambda i: r.gg.at[i], r.dg, (r.qs, r.qr, r.ql))
        back.start()
        u = Return(t, r, 'u', row, capacity, False)

        def work():
            shared.ready()
            shared.backward(r.xdy[:d], r.xdy[d:], r.ds)

        drive([u], work)
        r.dx[...] = (r.xdy[d:].astype(F32) + r.ds[...] + u.out[...]).astype(BF16)
        back.finish()

    res = run_kernel(body, cid, {**ins, **g_ins, **w_ins, 'by_x': (lines[0], VMEM), 'by_y': (lines[1], VMEM),
                                 'xdy': (block, VMEM)},
                     {**g_outs, 'dx': ((d, tokens), BF16, VMEM)},
                     {**scratch, **g_scratch, **w_scratch, 'ds': VMEM((d, tokens), F32)})
    return res.dx, res.dg


def swiglu_grads(pre_gate, pre_up, d_hidden):
    sigma = jax.nn.sigmoid(pre_gate)
    d_gate = d_hidden * pre_up * sigma * (1.0 + pre_gate * (1.0 - sigma))
    d_up = d_hidden * pre_gate * sigma
    return d_gate.astype(BF16), d_up.astype(BF16)


def gate_table(idx, gate, n_experts):
    ids = jnp.arange(n_experts, dtype=idx.dtype)[:, None, None]
    return jnp.sum(jnp.where(idx.T[None] == ids, gate.T[None], 0.0), axis=1)


def pair_gates(dg, idx):
    ids = jnp.arange(dg.shape[0], dtype=idx.dtype)[:, None, None]
    return jnp.sum(jnp.where(idx.T[None] == ids, dg[:, None, :], 0.0), axis=0).T


def solution(mesh):
    n = mesh.shape['ep']
    token_spec = P(('dp', 'ep'), None)
    expert_spec = P('ep', None, None)
    shared_spec = P(None, None)
    grad_spec = P(('dp', 'ep'), None, None)
    layer_specs = (expert_spec,) * 3 + (shared_spec,) * 3

    def device_step(x_in, d_out, idx_a, gate_a, idx_b, gate_b,
                    w1_a, w3_a, w2_a, ws1_a, ws3_a, ws2_a,
                    w1_b, w3_b, w2_b, ws1_b, ws3_b, ws2_b):
        tokens, top_k = idx_a.shape
        n_experts = w1_a.shape[0] * n
        capacity = top_k * ((2 * tokens + n_experts - 1) // n_experts)

        flip = lambda w: jnp.swapaxes(w, 1, 2)
        w1_a, w3_a, w1_b, w3_b = flip(w1_a), flip(w3_a), flip(w1_b), flip(w3_b)

        odd = lax.rem(lax.axis_index('ep'), 2) == 1
        tables = [gate_table(i, g, n_experts).reshape(n, 2, tokens) for i, g in ((idx_a, gate_a), (idx_b, gate_b))]
        tables = [jnp.where(odd, t[:, ::-1], t) for t in tables]
        g_own = jnp.concatenate(tables + [jnp.zeros((n, 4, tokens), F32)], axis=1)

        x_t, dy_t = x_in.T, d_out.T
        shared_a, shared_b = (ws1_a, ws3_a, ws2_a), (ws1_b, ws3_b, ws2_b)
        xg, g_recv, lines, s_a = gather_first(x_t, g_own, shared_a, n, 0)
        (o_a,) = experts_forward(xg, g_recv, w1_a, w3_a, w2_a, 0, capacity, False)
        block = return_first(o_a, lines, x_t, s_a, dy_t, 0, capacity, n, 1)

        both, s_b, ds_b = gather_second(block, shared_b, n, 2)
        o_b, rows_b = experts_forward(both, g_recv, w1_b, w3_b, w2_b, 2, capacity, True)
        dw1_b, dw3_b, dw2_b, du_b, gg_b = experts_backward(rows_b, both, g_recv, w1_b, w3_b, w2_b, 2, capacity, True)
        x_last, block, dg_b = return_second(du_b, o_b, gg_b, lines, block, s_b, ds_b, x_t, 2, capacity, n, 3)

        both = gather_third(block, n, 4)
        dw1_a, dw3_a, dw2_a, du_a, gg_a = experts_backward(both, both, g_recv, w1_a, w3_a, w2_a, 0, capacity, False)
        d_first, dg_a = return_third(du_a, gg_a, lines, block, shared_a, 0, capacity, n, 5)
        x_last, d_first = x_last.T, d_first.T

        def unswap(dg):
            return jnp.where(odd, dg[:, ::-1], dg).reshape(2 * n, tokens)

        return (x_last, d_first, flip(dw1_a), flip(dw3_a), dw2_a, flip(dw1_b), flip(dw3_b), dw2_b,
                pair_gates(unswap(dg_a), idx_a), pair_gates(unswap(dg_b), idx_b))

    in_specs = (token_spec,) * 6 + layer_specs + layer_specs
    out_specs = (token_spec, token_spec) + (grad_spec,) * 6 + (token_spec, token_spec)
    return jax.shard_map(device_step, mesh=mesh, in_specs=in_specs, out_specs=out_specs, check_vma=False)
```

time: 858 us -> 389 us (0.45)
  Pallas kernels: 0 us -> 374 us
  local copies, waits for them, and re-layouts: 341 us -> 4.95 us
  other arithmetic: 179 us -> 3.98 us
  matrix products: 115 us -> 0 us
  starting transfers between devices: 83.2 us -> 0 us
  waiting for transfers between devices: 65.4 us -> 0 us
  blocking collectives: 59.1 us -> 0 us
    pallas_call x0 -> x10, Pallas kernels: none -> 374 us  [the longest x6 290 us: run_kernel(): pl.pallas_call(kernel, out_shape=[jax.ShapeDtypeStruct(shape, dtype) for...]
    gather x24 -> x0, local copies, waits for them, and re-layouts: 234 us -> none  [the longest x4 46.2 us: layer_backward(): gates.reshape(-1)[src_pair]]
    dot_general x30 -> x0, matrix products: 115 us -> none  [the longest x2 16.2 us: layer_backward(): jnp.einsum('erd,efd->erf', dy_rows, w_down, preferred_element_type=jnp.fl...]
    gather x12 -> x0, other arithmetic: 83.8 us -> none  [the longest x2 72.3 us: layer_forward(): per_pair = returned[tables[2]].reshape(tokens, top_k, -1)]
    all_to_all x11 -> x0, starting transfers between devices: 83.2 us -> none  [the longest x6 46.3 us: to_sources(): received = lax.all_to_all(shaped, 'ep', 2, 0, tiled=True)]
    all_to_all x11 -> x0, waiting for transfers between devices: 65.4 us -> none  [the longest x6 40.2 us: to_sources(): received = lax.all_to_all(shaped, 'ep', 2, 0, tiled=True)]
    all_to_all x1 -> x0, blocking collectives: 59.1 us -> none  [to_experts(): received = lax.all_to_all(shaped, 'ep', 0, 2, tiled=True)]
    reshape x12 -> x2, local copies, waits for them, and re-layouts: 46.3 us -> 0.08 us  [device_step(): gate_table(i, g, n_experts).reshape(n, 2, tokens)]
  transfers between devices with their start and end apart: 11 -> 0, of which waited for: 5 -> 0; matrix products, arithmetic and copies ran while one was open for 58% -> 0% of each run, Pallas kernels for 0% -> 0%
where the time goes in v2:
time: 389 us; the launch traced here: 384 us
  Pallas kernels  374 us (96%)
  local copies, waits for them, and re-layouts  4.95 us (1%)
  other arithmetic  3.98 us (1%)
    pallas_call x6, Pallas kernels, run_kernel(): pl.pallas_call(kernel, out_shape=[jax.ShapeDtypeStruct(shape, dtype) for...  290 us
    pallas_call x2, Pallas kernels, experts_backward(): pl.pallas_call(functools.partial(backward_kernel, row, capacity, kept), g...  53.1 us
    pallas_call x2, Pallas kernels, experts_forward(): pl.pallas_call(functools.partial(forward_kernel, row, capacity, keep), gr...  30.9 us

profile of v2, /device:TPU:97, one launch (start us, length us, event | category | flops | bytes accessed | tf_op | source)
XLA Modules:
  0.0 384.4 jit_solution(2157477500600701264)
XLA Ops:
  0.7 0.1 pad.2.clone
  0.7 0.9 select_reduce_fusion.3
  1.7 0.2 rev.12
  1.9 0.9 select_reduce_fusion.2
  2.8 0.2 rev.13
  3.1 0.8 maximum_maximum_fusion
  3.9 40.5 %shard_map.249 = (bf16[32,448,256]{2,1,0:T(8,128)(2,1)}, f32[32,8,256]{2,1,0:T(8,128)}, f32[4,4,2,8,256]{4,3,2,1,0:T(8,128)}, f32[4,4,2,8,256]{4,3,2,1,0:T(8,128)}, f32[448,256]{1,0:T(8,128)}) custom-call(bf16[448,256]{1,0:T(8,128)(2,1)} %bitcast.45, bf16[448,2560]{1,0:T(8,128)(2,1)} %refs_2_.5, bf16[448,2560]{1,0:T(8,128)(2,1)} %refs_3_.1, ...), custom_call_target="tpu_custom_call" | custom-call | tf_op jit(solution)/shard_map/pallas_call | solution.py:75
  44.4 15.4 %shard_map.250 = bf16[32,448,128]{2,1,0:T(8,128)(2,1)} custom-call(bf16[32,448,256]{2,1,0:T(8,128)(2,1)} %get-tuple-element.35.x_ref, f32[32,8,256]{2,1,0:T(8,128)} %get-tuple-element.36.g_ref, bf16[2,320,448]{2,1,0:T(8,128)(2,1)} %bitcast.53, bf16[2,320,448]{2,1,0:T(8,128)(2,1)} %bitcast.55, bf16[2,320,448]{2,1,0:T(8,128)(2,1)} %w2_ref.7), custom_call_target="tpu_custom_call" | custom-call | tf_op jit(solution)/shard_map/pallas_call | solution.py:510
  59.8 38.9 %shard_map.251.refs_0_.refs_4_.refs_5_ = bf16[896,256]{1,0:T(8,128)(2,1)} custom-call(bf16[4,4,2,448,128]{4,3,2,1,0:T(8,128)(2,1)} %bitcast.39, f32[4,8,8,256]{3,2,1,0:T(8,128)} %bitcast.57, f32[4,8,8,256]{3,2,1,0:T(8,128)} %bitcast.60, bf16[448,256]{1,0:T(8,128)(2,1)} %bitcast.47, f32[448,256]{1,0:T(8,128)} %get-tuple-element.39.refs_4_, ...), custom_call_target="tpu_custom_call" | custom-call | tf_op jit(solution)/shard_map/pallas_call | solution.py:75
  98.7 54.9 %shard_map.252 = (bf16[32,896,256]{2,1,0:T(8,128)(2,1)}, f32[448,256]{1,0:T(8,128)}, f32[448,256]{1,0:T(8,128)}) custom-call(bf16[896,256]{1,0:T(8,128)(2,1)} %shard_map.251.refs_0_.refs_4_.refs_5_, bf16[448,2560]{1,0:T(8,128)(2,1)} %refs_1_.3, bf16[448,2560]{1,0:T(8,128)(2,1)} %refs_2_.4, bf16[448,2560]{1,0:T(8,128)(2,1)} %bitcast.63, ...), custom_call_target="tpu_custom_call" | custom-call | tf_op jit(solution)/shard_map/pallas_call | solution.py:75
  153.7 15.5 %shard_map.253 = (bf16[32,448,128]{2,1,0:T(8,128)(2,1)}, bf16[2,448,2048]{2,1,0:T(8,128)(2,1)}) custom-call(bf16[32,896,256]{2,1,0:T(8,128)(2,1)} %get-tuple-element.40.x_ref.dy_ref, f32[32,8,256]{2,1,0:T(8,128)} %get-tuple-element.36.g_ref, bf16[2,320,448]{2,1,0:T(8,128)(2,1)} %bitcast.49, bf16[2,320,448]{2,1,0:T(8,128)(2,1)} %bitcast.51, ...), custom_call_target="tpu_custom_call" | custom-call | tf_op jit(solution)/shard_map/pallas_call | solution.py:510
  169.2 25.4 %shard_map.254 = (f32[2,320,448]{2,1,0:T(8,128)}, f32[2,320,448]{2,1,0:T(8,128)}, f32[2,320,448]{2,1,0:T(8,128)}, bf16[32,448,128]{2,1,0:T(8,128)(2,1)}, f32[32,2,256]{2,1,0:T(2,128)}) custom-call(bf16[2,448,2048]{2,1,0:T(8,128)(2,1)} %get-tuple-element.41.x_ref, bf16[32,896,256]{2,1,0:T(8,128)(2,1)} %get-tuple-element.40.x_ref.dy_ref, ...), custom_call_target="tpu_custom_call" | custom-call | tf_op jit(solution)/shard_map/pallas_call | solution.py:529
  194.5 70.5 %shard_map.255 = (f32[32,2,256]{2,1,0:T(2,128)}, bf16[448,256]{1,0:T(8,128)(2,1)}, bf16[896,256]{1,0:T(8,128)(2,1)}) custom-call(bf16[4,4,2,448,128]{4,3,2,1,0:T(8,128)(2,1)} %bitcast.43, bf16[4,4,2,448,128]{4,3,2,1,0:T(8,128)(2,1)} %bitcast.42, f32[32,2,256]{2,1,0:T(2,128)} %get-tuple-element.44.refs_2_, f32[4,8,8,256]{3,2,1,0:T(8,128)} %bitcast.58, ...), custom_call_target="tpu_custom_call" | custom-call | tf_op jit(solution)/shard_map/pallas_call | solution.py:75
  265.0 0.9 rev.15
  266.0 44.3 %shard_map.256.x_ref.dy_ref = bf16[32,896,256]{2,1,0:T(8,128)(2,1)} custom-call(bf16[896,256]{1,0:T(8,128)(2,1)} %get-tuple-element.48.refs_0_.refs_7_), custom_call_target="tpu_custom_call" | custom-call | tf_op jit(solution)/shard_map/pallas_call | solution.py:75
  310.3 27.7 %shard_map.257 = (f32[2,320,448]{2,1,0:T(8,128)}, f32[2,320,448]{2,1,0:T(8,128)}, f32[2,320,448]{2,1,0:T(8,128)}, bf16[32,448,128]{2,1,0:T(8,128)(2,1)}, f32[32,2,256]{2,1,0:T(2,128)}) custom-call(bf16[32,896,256]{2,1,0:T(8,128)(2,1)} %shard_map.256.x_ref.dy_ref, bf16[32,896,256]{2,1,0:T(8,128)(2,1)} %shard_map.256.x_ref.dy_ref, ...), custom_call_target="tpu_custom_call" | custom-call | tf_op jit(solution)/shard_map/pallas_call | solution.py:529
  338.0 0.0 copy-start.2
  338.0 0.0 copy-start.3
  338.0 41.1 %shard_map.258 = (f32[32,2,256]{2,1,0:T(2,128)}, bf16[448,256]{1,0:T(8,128)(2,1)}) custom-call(bf16[4,4,2,448,128]{4,3,2,1,0:T(8,128)(2,1)} %bitcast.44, f32[32,2,256]{2,1,0:T(2,128)} %get-tuple-element.50.refs_1_, bf16[448,2560]{1,0:T(8,128)(2,1)} %refs_2_.5, bf16[448,2560]{1,0:T(8,128)(2,1)} %refs_3_.1, bf16[448,2560]{1,0:T(8,128)(2,1)} %bitcast.41, ...), custom_call_target="tpu_custom_call" | custom-call | tf_op jit(solution)/shard_map/pallas_call | solution.py:75
  379.2 0.9 rev.14
  380.2 0.7 select_reduce_fusion.1
  381.0 0.7 select_reduce_fusion
  381.7 0.7 copy.30
  382.3 1.6 copy.31
  (14 shorter events, 0.2 us)
Async XLA Ops:
  338.0 42.1 %copy-start = (f32[32,2,256]{2,1,0:T(2,128)S(1)}, f32[32,2,256]{2,1,0:T(2,128)}, u32[]{:S(2)}) copy-start(f32[32,2,256]{2,1,0:T(2,128)} %get-tuple-element.59) | copy-start | bytes 196612
  338.0 42.2 %copy-start.2 = (s32[256,8]{0,1:T(8,128)S(1)}, s32[256,8]{0,1:T(8,128)}, u32[]{:S(2)}) copy-start(s32[256,8]{0,1:T(8,128)} %param.20) | copy-start | bytes 24580
  338.0 42.9 %copy-start.3 = (s32[256,8]{0,1:T(8,128)S(1)}, s32[256,8]{0,1:T(8,128)}, u32[]{:S(2)}) copy-start(s32[256,8]{0,1:T(8,128)} %param.22) | copy-start | bytes 24580
  338.0 43.6 %copy-start.1 = (bf16[448,256]{1,0:T(8,128)(2,1)S(1)}, bf16[448,256]{1,0:T(8,128)(2,1)}, u32[]{:S(2)}) copy-start(bf16[448,256]{1,0:T(8,128)(2,1)} %get-tuple-element.47) | copy-start | bytes 688132

commit v3 on v2

v3 whole, which is shorter than its diff:
```python
import functools
import math
from types import SimpleNamespace

import jax
import jax.numpy as jnp
from jax import lax
from jax.experimental import pallas as pl
from jax.experimental.pallas import tpu as pltpu
from jax.sharding import PartitionSpec as P

MESH = pl.DeviceIdType.MESH
F32, BF16 = jnp.float32, jnp.bfloat16
NT = (((1,), (1,)), ((), ()))
VMEM_LIMIT = 62914560
PAIR = (0, 1)
SIDES = (1, -1)


def dev(i):
    return {'ep': i}


class Torus:
    def __init__(self, n):
        self.nx = math.isqrt(n // 2)
        self.ny = n // 2 // self.nx
        self.me = lax.axis_index('ep')
        self.c = lax.rem(self.me, 2)
        chip = self.me // 2
        self.x, self.y = lax.rem(chip, self.nx), chip // self.nx

    def at(self, dx, dy, c=None):
        x = lax.rem(self.x + dx + self.nx, self.nx)
        y = lax.rem(self.y + dy + self.ny, self.ny)
        return (y * self.nx + x) * 2 + (self.c if c is None else c)


def barrier_all(n):
    me = lax.axis_index('ep')
    b = pltpu.get_barrier_semaphore()

    def body(k, _):
        pl.semaphore_signal(b, inc=1, device_id=dev(lax.rem(me + k, n)), device_id_type=MESH)
        return 0

    lax.fori_loop(1, n, body, 0)
    pl.semaphore_wait(b, n - 1)


def remote(src, dst, ssem, rsem, to):
    return pltpu.make_async_remote_copy(src_ref=src, dst_ref=dst, send_sem=ssem, recv_sem=rsem,
                                        device_id=dev(to), device_id_type=MESH)


def barrier_some(partners):
    b = pltpu.get_barrier_semaphore()
    for p in partners:
        pl.semaphore_signal(b, inc=1, device_id=dev(p), device_id_type=MESH)
    pl.semaphore_wait(b, len(partners))


def around(t):
    return [t.at(*hops(h, d)) for h in PAIR for d in SIDES] + [t.at(0, 0, 1 - t.c)]


def lines_of(t):
    return [t.at(*hops(h, d), c) for h in PAIR for d in (1, -1, 2) for c in PAIR] + [t.at(0, 0, 1 - t.c)]


def run_kernel(body, cid, ins, outs, scratch):
    names = [*ins, *outs, *scratch]

    def kernel(*refs):
        body(SimpleNamespace(**dict(zip(names, refs))))

    spec = lambda space: pl.BlockSpec(memory_space=space)
    res = pl.pallas_call(
        kernel,
        out_shape=[jax.ShapeDtypeStruct(shape, dtype) for shape, dtype, _ in outs.values()],
        in_specs=[spec(space) for _, space in ins.values()],
        out_specs=[spec(space) for _, _, space in outs.values()],
        scratch_shapes=list(scratch.values()),
        compiler_params=pltpu.CompilerParams(collective_id=cid, has_side_effects=True, vmem_limit_bytes=VMEM_LIMIT),
    )(*[array for array, _ in ins.values()])
    return SimpleNamespace(**dict(zip(outs, res)))


RING = 4
HBM, VMEM = pl.ANY, pltpu.VMEM
dma = pltpu.SemaphoreType.DMA


def hops(h, d, e=0):
    return (d, e) if h == 0 else (e, d)


class Gather:
    def __init__(self, torus, r, rows):
        self.t, self.block, self.out, self.ssem, self.rsem, self.lsem = torus, r.block, r.gathered, r.gs, r.gr, r.gl
        self.half, self.quarter = rows // 2, rows // 4
        self.count, self.sent, self.sibling, self.m = 0, [], [], {}

    def ref(self, off, r0, nr, core=None):
        return self.out.at[self.t.at(*off, core), pl.ds(r0, nr), :]

    def send(self, off, r0, nr, to):
        i = self.count
        self.count += 1
        ref = self.ref(off, r0, nr)
        src = self.block.at[pl.ds(r0, nr), :] if off == (0, 0) else ref
        cp = remote(src, ref, self.ssem.at[i], self.rsem.at[i], to)
        cp.start()
        self.sent.append(cp)
        return i

    def move(self, off, r0, nr, to):
        return self.send(off, r0, nr, self.t.at(*to)), nr

    def arrive(self, ref, i):
        remote(ref, ref, self.ssem.at[i], self.rsem.at[i], self.t.at(1, 0)).wait_recv()

    def wait(self, off, r0, mv):
        self.arrive(self.ref(off, r0, mv[1]), mv[0])

    def to_sibling(self, off, r0, nr):
        self.sibling.append((off, r0, nr, self.send(off, r0, nr, self.t.at(0, 0, 1 - self.t.c))))

    def start(self):
        m, half = self.m, self.half
        for h in PAIR:
            for d in SIDES:
                m[h, 'own', d] = self.move((0, 0), h * half, half, hops(h, d))
        for h in PAIR:
            for d in SIDES:
                m[h, 0, d] = self.move((0, 0), h * half, half, hops(h, 0, d))
        self.to_sibling((0, 0), 0, half * 2)
        self.own = pltpu.make_async_copy(self.block, self.out.at[self.t.me], self.lsem.at[0])
        self.own.start()

    def across(self, h, b):
        for k, e in enumerate(SIDES):
            off = hops(h, b, -e)
            self.wait(off, h * self.half, self.m[h, b, e])
            self.m[h, b, e, 'on'] = self.move(off, h * self.half + k * self.quarter, self.quarter, hops(h, 0, e))
            self.to_sibling(off, h * self.half, self.half)

    def spread(self, h, b):
        for e in SIDES:
            self.m[h, b, e] = self.move(hops(h, b), h * self.half, self.half, hops(h, 0, e))
        self.to_sibling(hops(h, b), h * self.half, self.half)

    def run(self):
        m, half, q = self.m, self.half, self.quarter
        for h in PAIR:
            for k, d in enumerate(SIDES):
                self.wait(hops(h, -d), h * half, m[h, 'own', d])
                m[h, 'on', d] = self.move(hops(h, -d), h * half + k * q, q, hops(h, d))
                self.spread(h, -d)
        for h in PAIR:
            self.across(h, 0)
        for h in PAIR:
            for k, d in enumerate(SIDES):
                self.wait(hops(h, -2 * d), h * half + k * q, m[h, 'on', d])
            self.spread(h, 2)
        for b in (-1, 1, 2):
            for h in PAIR:
                self.across(h, b)
        for b in (0, -1, 1, 2):
            for h in PAIR:
                for k, e in enumerate(SIDES):
                    self.wait(hops(h, b, -2 * e), h * half + k * q, m[h, b, e, 'on'])
                self.to_sibling(hops(h, b, 2), h * half, half)

    def finish(self):
        for off, r0, nr, i in self.sibling:
            self.arrive(self.ref(off, r0, nr, 1 - self.t.c), i)
        for cp in self.sent:
            cp.wait_send()
        self.own.wait()


def gather_parts(block, n):
    sems = dma((80,))
    return ({'block': (block, HBM)}, {'gathered': ((n,) + block.shape, block.dtype, HBM)},
            {'gs': sems, 'gr': sems, 'gl': dma((1,))})


class Exchange:
    def __init__(self, t, n, src, dst, sems):
        self.t, self.n, self.src, self.dst = t, n, src, dst
        self.ss, self.rs, self.ls = sems

    def send(self, k):
        to = lax.rem(self.t.me + k, self.n)
        return remote(self.src(to), self.dst.at[self.t.me], self.ss.at[k], self.rs.at[k], to)

    def start(self):
        def body(k, _):
            self.send(k).start()
            return 0

        self.own = pltpu.make_async_copy(self.src(self.t.me), self.dst.at[self.t.me], self.ls.at[0])
        self.own.start()
        lax.fori_loop(1, self.n, body, 0)

    def finish(self):
        def body(k, _):
            fr = lax.rem(self.t.me - k + self.n, self.n)
            remote(self.src(fr), self.dst.at[fr], self.ss.at[k], self.rs.at[k], fr).wait_recv()
            self.send(k).wait_send()
            return 0

        lax.fori_loop(1, self.n, body, 0)
        self.own.wait()


class Tables:
    def __init__(self, t, n, r):
        self.t, self.r = t, r
        flat = lambda i: r.g.at[i // (2 * t.nx), lax.rem(i // 2, t.nx), lax.rem(i, 2)]
        self.experts = Exchange(t, n, flat, r.g_recv, (r.ts, r.tr, r.tl))

    def start(self):
        t, r = self.t, self.r
        by_x, by_y = r.lines.at[0], r.lines.at[1]
        self.own = [pltpu.make_async_copy(r.g.at[t.y], by_x.at[t.y], r.tl.at[1]),
                    pltpu.make_async_copy(r.g.at[:, t.x], by_y.at[t.x], r.tl.at[2])]
        for cp in self.own:
            cp.start()
        self.lines = []
        for d in range(1, RING):
            y, x = lax.rem(t.y + d, RING), lax.rem(t.x + d, RING)
            fy, fx = lax.rem(t.y + RING - d, RING), lax.rem(t.x + RING - d, RING)
            for h, src, dst, me, fr in ((1, r.g.at[y], by_x, t.y, fy), (0, r.g.at[:, x], by_y, t.x, fx)):
                self.lines += [remote(src, dst.at[i], r.us.at[h, d], r.ur.at[h, d], t.at(*hops(h, d))) for i in (me, fr)]
        for cp in self.lines[::2]:
            cp.start()
        self.experts.start()

    def finish(self):
        self.experts.finish()
        for cp, arrival in zip(self.lines[::2], self.lines[1::2]):
            arrival.wait_recv()
            cp.wait_send()
        for cp in self.own:
            cp.wait()


CHUNK = 512


class Shared:
    def __init__(self, r):
        self.r = r
        self.copies = [pltpu.make_async_copy(a, b, r.wl.at[i])
                       for i, (a, b) in enumerate(((r.ws1, r.v1), (r.ws3, r.v3), (r.ws2, r.v2)))]
        for cp in self.copies:
            cp.start()

    def ready(self):
        for cp in self.copies:
            cp.wait()

    def loop(self, out, step):
        out[...] = jnp.zeros_like(out)

        def body(i, _):
            out[...] += step(pl.ds(pl.multiple_of(i * CHUNK, CHUNK), CHUNK))
            return 0

        lax.fori_loop(0, self.r.v1.shape[1] // CHUNK, body, 0)

    def forward(self, x_t, out):
        r, x = self.r, x_t.T

        def step(at):
            return mm_nt(r.v2[:, at], hidden_of(mm(x, r.v1[:, at]), mm(x, r.v3[:, at]))[1])

        self.loop(out, step)

    def backward(self, x_t, dy_t, out):
        r, x, dy = self.r, x_t.T, dy_t.T

        def step(at):
            a1, a3 = mm(x, r.v1[:, at]), mm(x, r.v3[:, at])
            da1, da3 = swiglu_grads(a1, a3, mm(dy, r.v2[:, at]))
            return mm_nt(r.v1[:, at], da1) + mm_nt(r.v3[:, at], da3)

        self.loop(out, step)


def shared_parts(ws1, ws3, ws2):
    buf = VMEM(ws1.shape, BF16)
    return ({'ws1': (ws1, HBM), 'ws3': (ws3, HBM), 'ws2': (ws2.T, HBM)},
            {'v1': buf, 'v3': buf, 'v2': buf, 'wl': dma((3,))})


def gather_first(x_t, g, n, cid):
    tokens = g.shape[2]
    side = math.isqrt(n // 2)
    by = (side, side, 2, 8, tokens)
    ins, outs, scratch = gather_parts(x_t, n)
    table, lines = dma((n,)), dma((2, RING))

    def body(r):
        t = Torus(n)
        barrier_all(n)
        gather, tables = Gather(t, r, x_t.shape[0]), Tables(t, n, r)
        gather.start()
        tables.start()
        gather.run()
        tables.finish()
        gather.finish()

    res = run_kernel(body, cid, {**ins, 'g': (g.reshape(by), HBM)},
                     {**outs, 'g_recv': ((n, 8, tokens), F32, HBM), 'lines': ((2,) + by, F32, HBM)},
                     {**scratch, 'ts': table, 'tr': table, 'tl': dma((3,)), 'us': lines, 'ur': lines})
    return res.gathered, res.g_recv, res.lines.reshape(2, side, 2 * side, 8, tokens)


def gather_block(block, n, cid):
    ins, outs, scratch = gather_parts(block, n)

    def body(r):
        t = Torus(n)
        barrier_some(around(t))
        gather = Gather(t, r, block.shape[0])
        gather.start()
        gather.run()
        gather.finish()

    return run_kernel(body, cid, ins, outs, scratch).gathered


class Late:
    def __init__(self, r, capacity):
        self.r, self.capacity = r, capacity
        self.copies = [pltpu.make_async_copy(a, b, r.el.at[i]) for i, (a, b) in
                       enumerate(((r.rows, r.rv), (r.w1, r.u1), (r.w3, r.u3), (r.w2, r.u2)))]
        for cp in self.copies:
            cp.start()

    def run(self):
        r = self.r
        width = 2 * self.capacity
        for cp in self.copies:
            cp.wait()
        for e in PAIR:
            r.u2t[e] = r.u2[e].T

        def body(i, _):
            o = []
            for e in PAIR:
                rows = r.rv[e, :, pl.ds(pl.multiple_of(i * 4 * width, 4 * width), 4 * width)]
                o.append(mm(r.u2t[e], hidden_of(mm(r.u1[e], rows), mm(r.u3[e], rows))[1]))
            for p in range(4):
                halves = swap_halves(*[v[:, p * width:(p + 1) * width] for v in o])
                for k in PAIR:
                    r.ov[8 * i + 2 * p + k] = halves[k].astype(BF16)
            return 0

        lax.fori_loop(0, r.rv.shape[2] // (4 * width), body, 0)
        self.out = pltpu.make_async_copy(r.ov, r.o, r.el.at[0])
        self.out.start()

    def finish(self):
        self.out.wait()


def late_parts(rows, weights, capacity, n):
    d, w = rows.shape[1], VMEM(weights[0].shape, BF16)
    sends = (n, d, 2 * capacity)
    return ({'rows': (rows, HBM), **{k: (v, HBM) for k, v in zip(('w1', 'w3', 'w2'), weights)}},
            {'o': (sends, BF16, HBM)},
            {'rv': VMEM(rows.shape, BF16), 'u1': w, 'u3': w, 'u2': w, 'u2t': VMEM((2, d, w.shape[1]), BF16),
             'ov': VMEM(sends, BF16), 'el': dma((4,))})


def mm(a, b):
    return jnp.dot(a, b, preferred_element_type=F32)


def mm_nt(a, b):
    return lax.dot_general(a, b, NT, preferred_element_type=F32)


def slots_of(gates):
    tokens = gates.shape[1]
    before = (lax.broadcasted_iota(jnp.int32, (tokens, tokens), 0)
              < lax.broadcasted_iota(jnp.int32, (tokens, tokens), 1))
    member = gates > 0.0
    count = mm(jnp.where(member, 1.0, 0.0).astype(BF16), jnp.where(before, 1.0, 0.0).astype(BF16))
    return jnp.where(member, count, -1.0)


def pick(slot_rows, capacity):
    tokens = slot_rows[0].shape[1]
    want = lax.broadcasted_iota(jnp.int32, (capacity, tokens), 0).astype(F32)
    return jnp.concatenate([jnp.where(s == want, 1.0, 0.0) for s in slot_rows], axis=0)


def split3(v):
    a = v.astype(BF16).astype(F32)
    r = v - a
    b = r.astype(BF16).astype(F32)
    return a, b, r - b


def swap_halves(first, second):
    low = lax.broadcasted_iota(jnp.int32, first.shape, 1) < first.shape[1] // 2
    return jnp.where(low, first, second), jnp.where(low, second, first)


def hidden_of(a1, a3):
    sigma = jax.nn.sigmoid(a1)
    return sigma, (a1 * sigma * a3).astype(BF16)


def source_hot(slots, s, row, capacity):
    return pick([slots[8 * s + row:8 * s + row + 1], slots[8 * s + row + 1:8 * s + row + 2]], capacity).astype(BF16)


def pair_rows(block, p, slots, row, capacity):
    return swap_halves(*[mm_nt(block[s], source_hot(slots, s, row, capacity)) for s in (2 * p, 2 * p + 1)])


def forward_kernel(row, capacity, x_ref, g_ref, w1_ref, w3_ref, w2_ref, o_ref, w2t):
    sources = x_ref.shape[0]

    @pl.when(pl.program_id(0) == 0)
    def _():
        for e in PAIR:
            w2t[e] = w2_ref[e].T

    slots = slots_of(g_ref[...].reshape(sources * 8, -1))
    pairs = [pair_rows(x_ref, p, slots, row, capacity) for p in range(sources // 2)]
    o = []
    for e in PAIR:
        rows = jnp.concatenate([pr[e].astype(BF16) for pr in pairs], axis=1)
        hidden = hidden_of(mm(w1_ref[e], rows), mm(w3_ref[e], rows))[1]
        o.append(mm(w2t[e], hidden))
    width = 2 * capacity
    for p in range(sources // 2):
        a, b = swap_halves(o[0][:, p * width:(p + 1) * width], o[1][:, p * width:(p + 1) * width])
        o_ref[2 * p] = a.astype(BF16)
        o_ref[2 * p + 1] = b.astype(BF16)


def backward_kernel(row, capacity, keep, x_ref, dy_ref, g_ref, w1_ref, w3_ref, w2_ref,
                    dw1_ref, dw3_ref, dw2_ref, du_ref, gg_ref, *rest):
    w1n, w3n = rest[-2:]
    sources = dy_ref.shape[0]

    @pl.when(pl.program_id(0) == 0)
    def _():
        for ref in (dw1_ref, dw3_ref, dw2_ref):
            ref[...] = jnp.zeros_like(ref)
        for e in PAIR:
            w1n[e] = w1_ref[e].T
            w3n[e] = w3_ref[e].T

    d, tokens = dy_ref.shape[1:]
    width = 2 * capacity
    slots = slots_of(g_ref[...].reshape(sources * 8, -1))
    low = lax.broadcasted_iota(jnp.int32, (1, width), 1) < capacity
    hots, xp, dyp, gp = [], [], [], []
    for p in range(sources // 2):
        raw, gates, picked = [], [], []
        for s in (2 * p, 2 * p + 1):
            hot = source_hot(slots, s, row, capacity)
            hots.append(hot)
            picked.append(mm_nt(x_ref[s], hot))
            parts = split3(g_ref[s])
            extra = jnp.concatenate(list(parts) + [jnp.zeros_like(parts[0])], axis=0).astype(BF16)
            r = mm_nt(jnp.concatenate([dy_ref[s], extra], axis=0), hot)
            raw.append(r[:d])
            both = [r[d + i:d + i + 1] + r[d + 8 + i:d + 9 + i] + r[d + 16 + i:d + 17 + i] for i in (row, row + 1)]
            gates.append(jnp.where(low, *both))
        xp.append(swap_halves(*picked))
        dyp.append(swap_halves(*raw))
        gp.append(swap_halves(*gates))
    du, gg = [], []
    for e in PAIR:
        rows = jnp.concatenate([pr[e].astype(BF16) for pr in xp], axis=1)
        if keep:
            rest[0][e] = rows
        dy = jnp.concatenate([pr[e] for pr in dyp], axis=1)
        gate = jnp.concatenate([pr[e] for pr in gp], axis=1)
        a1, a3 = mm(w1_ref[e], rows), mm(w3_ref[e], rows)
        sigma, hidden = hidden_of(a1, a3)
        p32 = mm(w2_ref[e], dy.astype(BF16))
        gg.append(jnp.sum(hidden.astype(F32) * p32, axis=0, keepdims=True))
        dw2_ref[e] += mm_nt(hidden, (gate * dy).astype(BF16))
        q = gate * p32
        da1 = (q * a3 * sigma * (1.0 + a1 * (1.0 - sigma))).astype(BF16)
        da3 = (q * a1 * sigma).astype(BF16)
        dw1_ref[e] += mm_nt(da1, rows)
        dw3_ref[e] += mm_nt(da3, rows)
        du.append(mm(w1n[e], da1) + mm(w3n[e], da3))
    for p in range(sources // 2):
        at = slice(p * width, (p + 1) * width)
        for s, v in zip((2 * p, 2 * p + 1), swap_halves(du[0][:, at], du[1][:, at])):
            du_ref[s] = v.astype(BF16)
        for s, v in zip((2 * p, 2 * p + 1), swap_halves(gg[0][:, at], gg[1][:, at])):
            wide = jnp.broadcast_to(v, (8, width))
            expert = lax.broadcasted_iota(jnp.int32, (8, width), 0)
            block = lax.broadcasted_iota(jnp.int32, (8, width), 1) // capacity
            own = block == (expert if s % 2 == 0 else 1 - expert)
            parts = split3(jnp.where(own, wide, 0.0))
            res = mm(jnp.concatenate(list(parts) + [jnp.zeros_like(parts[0])], axis=0).astype(BF16), hots[s])
            gg_ref[s] = (res[:8] + res[8:16] + res[16:24])[:gg_ref.shape[1]]


SOURCES = 8


def whole(a):
    return pl.BlockSpec(a.shape, lambda i: (0,) * a.ndim)


def experts_forward(xg, gr, w1, w3, w2, row, capacity):
    n, tokens, d = xg.shape[0], xg.shape[2], w1.shape[2]
    grouped = lambda i: (i, 0, 0)
    return pl.pallas_call(
        functools.partial(forward_kernel, row, capacity),
        grid=(n // SOURCES,),
        out_shape=jax.ShapeDtypeStruct((n, d, 2 * capacity), BF16),
        out_specs=pl.BlockSpec((SOURCES, d, 2 * capacity), grouped),
        in_specs=[pl.BlockSpec((SOURCES, d, tokens), grouped), pl.BlockSpec((SOURCES, 8, tokens), grouped),
                  whole(w1), whole(w3), whole(w2)],
        scratch_shapes=[pltpu.VMEM((2, d, w2.shape[1]), BF16)],
        compiler_params=pltpu.CompilerParams(vmem_limit_bytes=VMEM_LIMIT),
    )(xg, gr, w1, w3, w2)


def experts_backward(both, gr, w1, w3, w2, row, capacity, keep):
    n, tokens, d = both.shape[0], both.shape[2], w1.shape[2]
    f = w2.shape[1]
    grouped = lambda i: (i, 0, 0)
    grads = [jax.ShapeDtypeStruct((2, f, d), F32)] * 3
    kept = [jax.ShapeDtypeStruct((2, d, n * capacity), BF16)] if keep else []
    return pl.pallas_call(
        functools.partial(backward_kernel, row, capacity, keep),
        grid=(n // SOURCES,),
        out_shape=grads + [jax.ShapeDtypeStruct((n, d, 2 * capacity), BF16),
                           jax.ShapeDtypeStruct((n, 2, tokens), F32)] + kept,
        out_specs=[whole(g) for g in grads] + [pl.BlockSpec((SOURCES, d, 2 * capacity), grouped),
                                               pl.BlockSpec((SOURCES, 2, tokens), grouped)]
        + [pl.BlockSpec((2, d, SOURCES * capacity), lambda i: (0, 0, i)) for _ in kept],
        in_specs=[pl.BlockSpec((SOURCES, d, tokens), grouped), pl.BlockSpec((SOURCES, d, tokens), lambda i: (i, 1, 0)),
                  pl.BlockSpec((SOURCES, 8, tokens), grouped), whole(w1), whole(w3), whole(w2)],
        scratch_shapes=[pltpu.VMEM((2, d, f), BF16)] * 2,
        compiler_params=pltpu.CompilerParams(vmem_limit_bytes=VMEM_LIMIT),
    )(both, both, gr, w1, w3, w2)


FAR_TO_NEAR = (2, 1, -1, 0)
RETURN_SCRATCH = ('recv', 'part', 'fin', 'ss', 'rs', 'ss2', 'rs2', 'ls', 'slots', 'acc')


class Return:
    def __init__(self, torus, r, name, row, capacity, gated):
        self.t, self.row, self.capacity, self.gated = torus, row, capacity, gated
        for field in ('src', 'out', *RETURN_SCRATCH):
            setattr(self, field, getattr(r, name + field))
        self.tables = r.lines
        self.half = self.src.shape[3] // 2
        self.sent = []

    def pos(self, h):
        return (self.t.x, self.t.y) if h == 0 else (self.t.y, self.t.x)

    def source(self, h, p, q, core):
        rows = pl.ds(h * self.half, self.half)
        a, b = (q, p) if h == 0 else (p, q)
        return self.src.at[a, b, core, rows, :]

    def send(self, src, dst, ssem, rsem, to):
        cp = remote(src, dst, ssem, rsem, to)
        cp.start()
        self.sent.append(cp)

    def sends(self, j):
        c = self.t.c
        for h in PAIR:
            p, q0 = self.pos(h)
            q = lax.rem(q0 + FAR_TO_NEAR[j] + RING, RING)
            dst = self.recv.at[h, j, p * 2 + c]
            ss, rs = self.ss.at[h, j], self.rs.at[h, j]
            for i, d in enumerate((2, 1, -1)):
                for core in PAIR:
                    self.send(self.source(h, lax.rem(p + d + RING, RING), q, core), dst, ss.at[2 * i + core],
                              rs.at[2 * i + c], self.t.at(*hops(h, d), core))
            self.send(self.source(h, p, q, 1 - c), dst, ss.at[6], rs.at[6], self.t.at(0, 0, 1 - c))
            pltpu.make_async_copy(self.source(h, p, q, c), dst, self.ls.at[h, j]).start()

    def arrive(self, dst, sem):
        remote(dst, dst, sem, sem, self.t.at(1, 0)).wait_recv()

    def arrivals(self, j):
        for h in PAIR:
            dst = self.recv.at[h, j, 0]
            for slot in range(7):
                self.arrive(dst, self.rs.at[h, j, slot])
            pltpu.make_async_copy(dst, dst, self.ls.at[h, j]).wait()

    def combine(self, j):
        def half(h, _):
            q0 = jnp.where(h == 0, self.t.y, self.t.x)
            gates = self.tables.at[h, lax.rem(q0 + FAR_TO_NEAR[j] + RING, RING)]
            senders, rows, tokens = gates.shape
            self.slots[...] = slots_of(gates[...].reshape(senders * rows, tokens)).reshape(gates.shape)
            self.acc[...] = jnp.zeros_like(self.acc)

            def body(m, _):
                ks = [2 * m + i for i in PAIR]
                lhs = jnp.concatenate([self.recv[h, j, k] for k in ks], axis=1)
                pairs = [(k, pl.ds(self.row + e, 1)) for k in ks for e in PAIR]
                hot = pick([self.slots[at] for at in pairs], self.capacity)
                weights = [hot]
                if self.gated:
                    parts = [split3(gates[at]) for at in pairs]
                    weights = [hot * jnp.concatenate([jnp.broadcast_to(g, (self.capacity, tokens)) for g in part], axis=0)
                               for part in zip(*parts)]
                self.acc[...] += sum(mm(lhs, w.astype(BF16)) for w in weights)
                return 0

            lax.fori_loop(0, senders // 2, body, 0)
            self.part[h, j] = self.acc[...]
            return 0

        lax.fori_loop(0, 2, half, 0)

    def round(self, j):
        self.combine(j)
        if j < RING - 1:
            for h in PAIR:
                self.send(self.part.at[h, j], self.fin.at[h, j], self.ss2.at[h, j], self.rs2.at[h, j],
                          self.t.at(*hops(h, 0, FAR_TO_NEAR[j])))

    def finish(self):
        for h in PAIR:
            for j in range(RING - 1):
                self.arrive(self.fin.at[h, j], self.rs2.at[h, j])
            at = slice(h * self.half, (h + 1) * self.half)
            self.out[at, :] = self.part[h, RING - 1] + self.fin[h, 0] + self.fin[h, 1] + self.fin[h, 2]
        for cp in self.sent:
            cp.wait_send()


def return_parts(name, rows, tokens, n):
    d, width = rows.shape[1:]
    side = math.isqrt(n // 2)
    half = d // 2
    first, second = dma((2, RING, 7)), dma((2, RING))
    shapes = (VMEM((2, RING, 2 * RING, half, width), BF16), VMEM((2, RING, half, tokens), F32),
              VMEM((2, RING - 1, half, tokens), F32), first, first, second, second, second,
              VMEM((2 * RING, 8, tokens), F32), VMEM((half, tokens), F32))
    return ({name + 'src': (rows.reshape(side, side, 2, d, width), HBM)},
            {**{name + f: shape for f, shape in zip(RETURN_SCRATCH, shapes)}, name + 'out': VMEM((d, tokens), F32)})


def drive(todo, work):
    for r in todo:
        for j in range(RING):
            r.sends(j)
    work()
    for r in todo:
        for j in range(RING):
            r.arrivals(j)
            r.round(j)
    for r in todo:
        r.finish()


def gg_parts(gg, n):
    sems = dma((n,))
    return {'gg': (gg, HBM)}, {'dg': (gg.shape, F32, HBM)}, {'qs': sems, 'qr': sems, 'ql': dma((1,))}


def return_first(o, lines, x_t, dy_t, weights, row, capacity, n, cid):
    d, tokens = x_t.shape
    ins, scratch = return_parts('o', o, tokens, n)
    w_ins, w_scratch = shared_parts(*weights)

    def body(r):
        t = Torus(n)
        shared = Shared(r)
        barrier_some(lines_of(t))
        job = Return(t, r, 'o', row, capacity, True)

        def work():
            shared.ready()
            shared.forward(r.x[...], r.s)

        drive([job], work)
        r.block[:d] = (r.x[...].astype(F32) + r.s[...] + job.out[...]).astype(BF16)
        r.block[d:] = r.dy[...]

    return run_kernel(body, cid, {**ins, **w_ins, 'lines': (lines, VMEM), 'x': (x_t, VMEM), 'dy': (dy_t, VMEM)},
                      {'block': ((2 * d, tokens), BF16, VMEM)},
                      {**scratch, **w_scratch, 's': VMEM((d, tokens), F32)}).block


def return_second(du, gg, lines, block, x_t, rows, experts, weights, row, capacity, n, cid):
    d, tokens = x_t.shape
    ins, scratch = return_parts('u', du, tokens, n)
    g_ins, g_outs, g_scratch = gg_parts(gg, n)
    w_ins, w_scratch = shared_parts(*weights)
    l_ins, l_outs, l_scratch = late_parts(rows, experts, capacity, n)

    def body(r):
        t = Torus(n)
        shared, late = Shared(r), Late(r, capacity)
        barrier_all(n)
        back = Exchange(t, n, lambda i: r.gg.at[i], r.dg, (r.qs, r.qr, r.ql))
        back.start()
        u = Return(t, r, 'u', row, capacity, False)

        def work():
            late.run()
            shared.ready()
            shared.backward(r.x1dy[:d], r.x1dy[d:], r.ds)
            shared.forward(r.x1dy[:d], r.s)

        drive([u], work)
        r.block[:d] = r.x[...]
        r.block[d:] = (r.x1dy[d:].astype(F32) + r.ds[...] + u.out[...]).astype(BF16)
        back.finish()
        late.finish()

    res = run_kernel(body, cid, {**ins, **g_ins, **w_ins, **l_ins, 'lines': (lines, VMEM), 'x1dy': (block, VMEM),
                                 'x': (x_t, VMEM)},
                     {**g_outs, **l_outs, 'block': (block.shape, BF16, VMEM), 's': ((d, tokens), F32, VMEM)},
                     {**scratch, **g_scratch, **w_scratch, **l_scratch, 'ds': VMEM((d, tokens), F32)})
    return res.block, res.dg, res.o, res.s


def return_third(du, o, gg, lines, block, x1dy, s, weights, rows_of, capacity, n, cid):
    d, tokens = s.shape
    u_ins, u_scratch = return_parts('u', du, tokens, n)
    o_ins, o_scratch = return_parts('o', o, tokens, n)
    g_ins, g_outs, g_scratch = gg_parts(gg, n)
    w_ins, w_scratch = shared_parts(*weights)

    def body(r):
        t = Torus(n)
        shared = Shared(r)
        barrier_all(n)
        back = Exchange(t, n, lambda i: r.gg.at[i], r.dg, (r.qs, r.qr, r.ql))
        back.start()
        u = Return(t, r, 'u', rows_of[0], capacity, False)
        o = Return(t, r, 'o', rows_of[1], capacity, True)

        def work():
            shared.ready()
            shared.backward(r.xdy[:d], r.xdy[d:], r.ds)

        drive([o, u], work)
        r.last[...] = (r.x1dy[:d].astype(F32) + r.s[...] + o.out[...]).astype(BF16)
        r.dx[...] = (r.xdy[d:].astype(F32) + r.ds[...] + u.out[...]).astype(BF16)
        back.finish()

    res = run_kernel(body, cid, {**u_ins, **o_ins, **g_ins, **w_ins, 'lines': (lines, VMEM),
                                 'xdy': (block, VMEM), 'x1dy': (x1dy, VMEM), 's': (s, VMEM)},
                     {**g_outs, 'dx': ((d, tokens), BF16, VMEM), 'last': ((d, tokens), BF16, VMEM)},
                     {**u_scratch, **o_scratch, **g_scratch, **w_scratch, 'ds': VMEM((d, tokens), F32)})
    return res.dx, res.last, res.dg


def swiglu_grads(pre_gate, pre_up, d_hidden):
    sigma = jax.nn.sigmoid(pre_gate)
    d_gate = d_hidden * pre_up * sigma * (1.0 + pre_gate * (1.0 - sigma))
    d_up = d_hidden * pre_gate * sigma
    return d_gate.astype(BF16), d_up.astype(BF16)


def gate_table(idx, gate, n_experts):
    ids = jnp.arange(n_experts, dtype=idx.dtype)[:, None, None]
    return jnp.sum(jnp.where(idx.T[None] == ids, gate.T[None], 0.0), axis=1)


def pair_gates(dg, idx):
    ids = jnp.arange(dg.shape[0], dtype=idx.dtype)[:, None, None]
    return jnp.sum(jnp.where(idx.T[None] == ids, dg[:, None, :], 0.0), axis=0).T


def solution(mesh):
    n = mesh.shape['ep']
    token_spec = P(('dp', 'ep'), None)
    expert_spec = P('ep', None, None)
    shared_spec = P(None, None)
    grad_spec = P(('dp', 'ep'), None, None)
    layer_specs = (expert_spec,) * 3 + (shared_spec,) * 3

    def device_step(x_in, d_out, idx_a, gate_a, idx_b, gate_b,
                    w1_a, w3_a, w2_a, ws1_a, ws3_a, ws2_a,
                    w1_b, w3_b, w2_b, ws1_b, ws3_b, ws2_b):
        tokens, top_k = idx_a.shape
        n_experts = w1_a.shape[0] * n
        capacity = top_k * ((2 * tokens + n_experts - 1) // n_experts)

        flip = lambda w: jnp.swapaxes(w, 1, 2)
        w1_a, w3_a, w1_b, w3_b = flip(w1_a), flip(w3_a), flip(w1_b), flip(w3_b)

        odd = lax.rem(lax.axis_index('ep'), 2) == 1
        tables = [gate_table(i, g, n_experts).reshape(n, 2, tokens) for i, g in ((idx_a, gate_a), (idx_b, gate_b))]
        tables = [jnp.where(odd, t[:, ::-1], t) for t in tables]
        g_own = jnp.concatenate(tables + [jnp.zeros((n, 4, tokens), F32)], axis=1)

        x_t, dy_t = x_in.T, d_out.T
        shared_a, shared_b = (ws1_a, ws3_a, ws2_a), (ws1_b, ws3_b, ws2_b)
        xg, g_recv, lines = gather_first(x_t, g_own, n, 0)
        o_a = experts_forward(xg, g_recv, w1_a, w3_a, w2_a, 0, capacity)
        x1dy = return_first(o_a, lines, x_t, dy_t, shared_a, 0, capacity, n, 1)

        both = gather_block(x1dy, n, 2)
        experts_b = (w1_b, w3_b, w2_b)
        dw1_b, dw3_b, dw2_b, du_b, gg_b, rows_b = experts_backward(both, g_recv, *experts_b, 2, capacity, True)
        block, dg_b, o_b, s_b = return_second(du_b, gg_b, lines, x1dy, x_t, rows_b, experts_b, shared_b, 2, capacity, n, 3)

        both = gather_block(block, n, 4)
        dw1_a, dw3_a, dw2_a, du_a, gg_a = experts_backward(both, g_recv, w1_a, w3_a, w2_a, 0, capacity, False)
        d_first, x_last, dg_a = return_third(du_a, o_b, gg_a, lines, block, x1dy, s_b, shared_a, (0, 2), capacity, n, 5)
        x_last, d_first = x_last.T, d_first.T

        return (x_last, d_first, flip(dw1_a), flip(dw3_a), dw2_a, flip(dw1_b), flip(dw3_b), dw2_b,
                pair_gates(dg_a.reshape(n_experts, tokens), idx_a), pair_gates(dg_b.reshape(n_experts, tokens), idx_b))

    in_specs = (token_spec,) * 6 + layer_specs + layer_specs
    out_specs = (token_spec, token_spec) + (grad_spec,) * 6 + (token_spec, token_spec)
    return jax.shard_map(device_step, mesh=mesh, in_specs=in_specs, out_specs=out_specs, check_vma=False)
```

time: 389 us -> 348 us (0.89); the launches traced: 384 us -> 348 us
  Pallas kernels: 374 us -> 338 us
    pallas_call x4 -> x3, Pallas kernels: 84 us -> 60.9 us  [the longest x2 48.6 us: experts_backward(): pl.pallas_call(functools.partial(backward_kernel, row, capacity, keep), g...]
    pallas_call x6, Pallas kernels: 290 us -> 277 us  [run_kernel(): pl.pallas_call(kernel, out_shape=[jax.ShapeDtypeStruct(shape, dtype) for...]
where the time goes in v3:
time: 348 us
  Pallas kernels  338 us (97%)
  local copies, waits for them, and re-layouts  5.68 us (2%)
  other arithmetic  3.95 us (1%)
    pallas_call x6, Pallas kernels, run_kernel(): pl.pallas_call(kernel, out_shape=[jax.ShapeDtypeStruct(shape, dtype) for...  277 us
    pallas_call x2, Pallas kernels, experts_backward(): pl.pallas_call(functools.partial(backward_kernel, row, capacity, keep), g...  48.6 us
    pallas_call x1, Pallas kernels, experts_forward(): pl.pallas_call(functools.partial(forward_kernel, row, capacity), grid=(n...  12.2 us

profile of v3, /device:TPU:97, one launch (start us, length us, event | category | flops | bytes accessed | tf_op | source)
XLA Modules:
  0.0 347.9 jit_solution(7177232484787883923)
XLA Ops:
  0.7 0.1 pad.2.clone
  0.7 0.9 select_reduce_fusion.3
  1.7 0.2 rev.6
  1.9 0.9 select_reduce_fusion.2
  2.8 0.2 rev.7
  3.1 0.8 maximum_maximum_fusion
  3.9 38.7 %shard_map.249 = (bf16[32,448,256]{2,1,0:T(8,128)(2,1)}, f32[32,8,256]{2,1,0:T(8,128)}, f32[2,4,4,2,8,256]{5,4,3,2,1,0:T(8,128)}) custom-call(bf16[448,256]{1,0:T(8,128)(2,1)} %bitcast.50, f32[4,4,2,8,256]{4,3,2,1,0:T(8,128)} %bitcast.53), custom_call_target="tpu_custom_call" | custom-call | tf_op jit(solution)/shard_map/pallas_call | solution.py:78
  42.6 12.2 %shard_map.250 = bf16[32,448,128]{2,1,0:T(8,128)(2,1)} custom-call(bf16[32,448,256]{2,1,0:T(8,128)(2,1)} %get-tuple-element.31.x_ref, f32[32,8,256]{2,1,0:T(8,128)} %get-tuple-element.32.g_ref, bf16[2,320,448]{2,1,0:T(8,128)(2,1)} %bitcast.45, bf16[2,320,448]{2,1,0:T(8,128)(2,1)} %bitcast.47, bf16[2,320,448]{2,1,0:T(8,128)(2,1)} %w2_ref.5), custom_call_target="tpu_custom_call" | custom-call | tf_op jit(solution)/shard_map/pallas_call | solution.py:525
  54.9 38.0 %shard_map.251.refs_0_.refs_10_.refs_8_ = bf16[896,256]{1,0:T(8,128)(2,1)} custom-call(bf16[4,4,2,448,128]{4,3,2,1,0:T(8,128)(2,1)} %bitcast.32, bf16[448,2560]{1,0:T(8,128)(2,1)} %refs_3_.3, bf16[448,2560]{1,0:T(8,128)(2,1)} %refs_4_.1, bf16[448,2560]{1,0:T(8,128)(2,1)} %bitcast.33, f32[2,4,8,8,256]{4,3,2,1,0:T(8,128)} %bitcast.35, ...), custom_call_target="tpu_custom_call" | custom-call | tf_op jit(solution)/shard_map/pallas_call | solution.py:78
  92.9 44.1 %shard_map.252.x_ref.dy_ref = bf16[32,896,256]{2,1,0:T(8,128)(2,1)} custom-call(bf16[896,256]{1,0:T(8,128)(2,1)} %shard_map.251.refs_0_.refs_10_.refs_8_), custom_call_target="tpu_custom_call" | custom-call | tf_op jit(solution)/shard_map/pallas_call | solution.py:78
  137.0 24.5 %shard_map.253 = (f32[2,320,448]{2,1,0:T(8,128)}, f32[2,320,448]{2,1,0:T(8,128)}, f32[2,320,448]{2,1,0:T(8,128)}, bf16[32,448,128]{2,1,0:T(8,128)(2,1)}, f32[32,...) custom-call(bf16[32,896,256]{2,1,0:T(8,128)(2,1)} %shard_map.252.x_ref.dy_ref, ...), custom_call_target="tpu_custom_call" | custom-call | tf_op jit(solution)/shard_map/pallas_call | solution.py:543
  161.5 0.0 copy-start
  161.5 40.3 %shard_map.254 = (f32[32,2,256]{2,1,0:T(2,128)}, bf16[32,448,128]{2,1,0:T(8,128)(2,1)}, bf16[896,256]{1,0:T(8,128)(2,1)}, f32[448,256]{1,0:T(8,128)}) custom-call(bf16[4,4,2,448,128]{4,3,2,1,0:T(8,128)(2,1)} %bitcast.38, f32[32,2,256]{2,1,0:T(2,128)} %get-tuple-element.35.refs_1_, bf16[448,2560]{1,0:T(8,128)(2,1)} %refs_2_.3, bf16[448,2560]{1,0:T(8,128)(2,1)} %refs_3_.2, ...), custom_call_target="tpu_custom_call" | custom-call | tf_op jit(solution)/shard_map/pallas_call | solution.py:78
  201.8 0.9 broadcast_in_dim.57
  202.7 0.0 copy-done
  202.7 0.7 select_reduce_fusion
  203.4 44.4 %shard_map.255.x_ref.dy_ref = bf16[32,896,256]{2,1,0:T(8,128)(2,1)} custom-call(bf16[896,256]{1,0:T(8,128)(2,1)} %get-tuple-element.37.refs_0_.refs_7_), custom_call_target="tpu_custom_call" | custom-call | tf_op jit(solution)/shard_map/pallas_call | solution.py:78
  247.8 24.1 %shard_map.256 = (f32[2,320,448]{2,1,0:T(8,128)}, f32[2,320,448]{2,1,0:T(8,128)}, f32[2,320,448]{2,1,0:T(8,128)}, bf16[32,448,128]{2,1,0:T(8,128)(2,1)}, f32[32,2,256]{2,1,0:T(2,128)}) custom-call(bf16[32,896,256]{2,1,0:T(8,128)(2,1)} %shard_map.255.x_ref.dy_ref, bf16[32,896,256]{2,1,0:T(8,128)(2,1)} %shard_map.255.x_ref.dy_ref, ...), custom_call_target="tpu_custom_call" | custom-call | tf_op jit(solution)/shard_map/pallas_call | solution.py:543
  271.9 71.1 %shard_map.257 = (f32[32,2,256]{2,1,0:T(2,128)}, bf16[448,256]{1,0:T(8,128)(2,1)}, bf16[448,256]{1,0:T(8,128)(2,1)}) custom-call(bf16[4,4,2,448,128]{4,3,2,1,0:T(8,128)(2,1)} %bitcast.40, bf16[4,4,2,448,128]{4,3,2,1,0:T(8,128)(2,1)} %bitcast.39, f32[32,2,256]{2,1,0:T(2,128)} %get-tuple-element.40.refs_2_, bf16[448,2560]{1,0:T(8,128)(2,1)} %refs_3_.3, ...), custom_call_target="tpu_custom_call" | custom-call | tf_op jit(solution)/shard_map/pallas_call | solution.py:78
  343.0 0.9 broadcast_in_dim.55
  343.9 0.0 copy-done.1
  343.9 0.7 select_reduce_fusion.1
  344.6 1.6 copy.30
  346.3 1.6 copy.31
  (5 shorter events, 0.1 us)
Async XLA Ops:
  161.5 41.2 %copy-start = (s32[256,8]{0,1:T(8,128)S(1)}, s32[256,8]{0,1:T(8,128)}, u32[]{:S(2)}) copy-start(s32[256,8]{0,1:T(8,128)} %param.22) | copy-start | bytes 24580
  271.9 72.0 %copy-start.1 = (s32[256,8]{0,1:T(8,128)S(1)}, s32[256,8]{0,1:T(8,128)}, u32[]{:S(2)}) copy-start(s32[256,8]{0,1:T(8,128)} %param.20) | copy-start | bytes 24580

commit v4 on v3

--- a/solution.py
+++ b/solution.py
@@ -150,13 +150,15 @@
             self.m[h, b, e] = self.move(hops(h, b), h * self.half, self.half, hops(h, 0, e))
         self.to_sibling(hops(h, b), h * self.half, self.half)
 
-    def run(self):
+    def run(self, then=None):
         m, half, q = self.m, self.half, self.quarter
         for h in PAIR:
             for k, d in enumerate(SIDES):
                 self.wait(hops(h, -d), h * half, m[h, 'own', d])
                 m[h, 'on', d] = self.move(hops(h, -d), h * half + k * q, q, hops(h, d))
                 self.spread(h, -d)
+        if then:
+            then()
         for h in PAIR:
             self.across(h, 0)
         for h in PAIR:
@@ -224,15 +226,15 @@
     def start(self):
         t, r = self.t, self.r
         by_x, by_y = r.lines.at[0], r.lines.at[1]
-        self.own = [pltpu.make_async_copy(r.g.at[t.y], by_x.at[t.y], r.tl.at[1]),
-                    pltpu.make_async_copy(r.g.at[:, t.x], by_y.at[t.x], r.tl.at[2])]
+        self.own = [pltpu.make_async_copy(r.chips.at[t.y], by_x.at[t.y], r.tl.at[1]),
+                    pltpu.make_async_copy(r.chips.at[:, t.x], by_y.at[t.x], r.tl.at[2])]
         for cp in self.own:
             cp.start()
         self.lines = []
         for d in range(1, RING):
             y, x = lax.rem(t.y + d, RING), lax.rem(t.x + d, RING)
             fy, fx = lax.rem(t.y + RING - d, RING), lax.rem(t.x + RING - d, RING)
-            for h, src, dst, me, fr in ((1, r.g.at[y], by_x, t.y, fy), (0, r.g.at[:, x], by_y, t.x, fx)):
+            for h, src, dst, me, fr in ((1, r.chips.at[y], by_x, t.y, fy), (0, r.chips.at[:, x], by_y, t.x, fx)):
                 self.lines += [remote(src, dst.at[i], r.us.at[h, d], r.ur.at[h, d], t.at(*hops(h, d))) for i in (me, fr)]
         for cp in self.lines[::2]:
             cp.start()
@@ -300,6 +302,7 @@
     tokens = g.shape[2]
     side = math.isqrt(n // 2)
     by = (side, side, 2, 8, tokens)
+    chips = g[:, :4].reshape(side, side, 8, tokens)
     ins, outs, scratch = gather_parts(x_t, n)
     table, lines = dma((n,)), dma((2, RING))
 
@@ -308,15 +311,14 @@
         barrier_all(n)
         gather, tables = Gather(t, r, x_t.shape[0]), Tables(t, n, r)
         gather.start()
-        tables.start()
-        gather.run()
+        gather.run(tables.start)
         tables.finish()
         gather.finish()
 
-    res = run_kernel(body, cid, {**ins, 'g': (g.reshape(by), HBM)},
-                     {**outs, 'g_recv': ((n, 8, tokens), F32, HBM), 'lines': ((2,) + by, F32, HBM)},
+    res = run_kernel(body, cid, {**ins, 'g': (g.reshape(by), HBM), 'chips': (chips, HBM)},
+                     {**outs, 'g_recv': ((n, 8, tokens), F32, HBM), 'lines': ((2,) + chips.shape, F32, HBM)},
                      {**scratch, 'ts': table, 'tr': table, 'tl': dma((3,)), 'us': lines, 'ur': lines})
-    return res.gathered, res.g_recv, res.lines.reshape(2, side, 2 * side, 8, tokens)
+    return res.gathered, res.g_recv, res.lines
 
 
 def gather_block(block, n, cid):
@@ -609,14 +611,14 @@
         def half(h, _):
             q0 = jnp.where(h == 0, self.t.y, self.t.x)
             gates = self.tables.at[h, lax.rem(q0 + FAR_TO_NEAR[j] + RING, RING)]
-            senders, rows, tokens = gates.shape
-            self.slots[...] = slots_of(gates[...].reshape(senders * rows, tokens)).reshape(gates.shape)
+            chips, rows, tokens = gates.shape
+            self.slots[...] = slots_of(gates[...].reshape(chips * rows, tokens)).reshape(gates.shape)
             self.acc[...] = jnp.zeros_like(self.acc)
 
             def body(m, _):
                 ks = [2 * m + i for i in PAIR]
                 lhs = jnp.concatenate([self.recv[h, j, k] for k in ks], axis=1)
-                pairs = [(k, pl.ds(self.row + e, 1)) for k in ks for e in PAIR]
+                pairs = [(m, pl.ds(4 * i + self.row + e, 1)) for i in PAIR for e in PAIR]
                 hot = pick([self.slots[at] for at in pairs], self.capacity)
                 weights = [hot]
                 if self.gated:
@@ -626,7 +628,7 @@
                 self.acc[...] += sum(mm(lhs, w.astype(BF16)) for w in weights)
                 return 0
 
-            lax.fori_loop(0, senders // 2, body, 0)
+            lax.fori_loop(0, chips, body, 0)
             self.part[h, j] = self.acc[...]
             return 0
 
@@ -656,7 +658,7 @@
     first, second = dma((2, RING, 7)), dma((2, RING))
     shapes = (VMEM((2, RING, 2 * RING, half, width), BF16), VMEM((2, RING, half, tokens), F32),
               VMEM((2, RING - 1, half, tokens), F32), first, first, second, second, second,
-              VMEM((2 * RING, 8, tokens), F32), VMEM((half, tokens), F32))
+              VMEM((RING, 8, tokens), F32), VMEM((half, tokens), F32))
     return ({name + 'src': (rows.reshape(side, side, 2, d, width), HBM)},
             {**{name + f: shape for f, shape in zip(RETURN_SCRATCH, shapes)}, name + 'out': VMEM((d, tokens), F32)})
 

time: 348 us -> 347 us (level)
  no operation moved by 1% of the time
where the time goes in v4:
time: 347 us; the launch traced here: 346 us
  Pallas kernels  335 us (97%)
  local copies, waits for them, and re-layouts  6.38 us (2%)
  other arithmetic  4.01 us (1%)
    pallas_call x6, Pallas kernels, run_kernel(): pl.pallas_call(kernel, out_shape=[jax.ShapeDtypeStruct(shape, dtype) for...  274 us
    pallas_call x2, Pallas kernels, experts_backward(): pl.pallas_call(functools.partial(backward_kernel, row, capacity, keep), g...  48.7 us
    pallas_call x1, Pallas kernels, experts_forward(): pl.pallas_call(functools.partial(forward_kernel, row, capacity), grid=(n...  12.2 us

profile of v4, /device:TPU:97, one launch (start us, length us, event | category | flops | bytes accessed | tf_op | source)
XLA Modules:
  0.0 346.1 jit_solution(13583565028048918574)
XLA Ops:
  0.7 0.1 pad.4.clone
  0.7 0.9 select_reduce_fusion.3
  1.7 0.2 rev.6
  1.9 0.9 select_reduce_fusion.2
  2.8 0.2 rev.7
  3.1 0.1 pad_maximum_fusion
  3.2 0.7 reshape.53.refs_2_
  3.9 0.8 maximum_maximum_fusion
  4.7 37.0 %shard_map.249 = (bf16[32,448,256]{2,1,0:T(8,128)(2,1)}, f32[32,8,256]{2,1,0:T(8,128)}, f32[2,4,4,8,256]{4,3,2,1,0:T(8,128)}) custom-call(bf16[448,256]{1,0:T(8,128)(2,1)} %bitcast.46, f32[4,4,2,8,256]{4,3,2,1,0:T(8,128)} %bitcast.49, f32[4,4,8,256]{3,2,1,0:T(8,128)} %reshape.53.refs_2_), custom_call_target="tpu_custom_call" | custom-call | tf_op jit(solution)/shard_map/pallas_call | solution.py:78
  41.6 12.2 %shard_map.250 = bf16[32,448,128]{2,1,0:T(8,128)(2,1)} custom-call(bf16[32,448,256]{2,1,0:T(8,128)(2,1)} %get-tuple-element.31.x_ref, f32[32,8,256]{2,1,0:T(8,128)} %get-tuple-element.32.g_ref, bf16[2,320,448]{2,1,0:T(8,128)(2,1)} %bitcast.41, bf16[2,320,448]{2,1,0:T(8,128)(2,1)} %bitcast.43, bf16[2,320,448]{2,1,0:T(8,128)(2,1)} %w2_ref.5), custom_call_target="tpu_custom_call" | custom-call | tf_op jit(solution)/shard_map/pallas_call | solution.py:527
  53.9 37.4 %shard_map.251.refs_0_.refs_10_.refs_8_ = bf16[896,256]{1,0:T(8,128)(2,1)} custom-call(bf16[4,4,2,448,128]{4,3,2,1,0:T(8,128)(2,1)} %bitcast.31, bf16[448,2560]{1,0:T(8,128)(2,1)} %refs_3_.3, bf16[448,2560]{1,0:T(8,128)(2,1)} %refs_4_.1, bf16[448,2560]{1,0:T(8,128)(2,1)} %bitcast.32, f32[2,4,4,8,256]{4,3,2,1,0:T(8,128)} %get-tuple-element.33.refs_4_.refs_9_.refs_6_, ...), custom_call_target="tpu_custom_call" | custom-call | tf_op jit(solution)/shard_map/pallas_call | solution.py:78
  91.3 44.1 %shard_map.252.x_ref.dy_ref = bf16[32,896,256]{2,1,0:T(8,128)(2,1)} custom-call(bf16[896,256]{1,0:T(8,128)(2,1)} %shard_map.251.refs_0_.refs_10_.refs_8_), custom_call_target="tpu_custom_call" | custom-call | tf_op jit(solution)/shard_map/pallas_call | solution.py:78
  135.4 24.5 %shard_map.253 = (f32[2,320,448]{2,1,0:T(8,128)}, f32[2,320,448]{2,1,0:T(8,128)}, f32[2,320,448]{2,1,0:T(8,128)}, bf16[32,448,128]{2,1,0:T(8,128)(2,1)}, f32[32,...) custom-call(bf16[32,896,256]{2,1,0:T(8,128)(2,1)} %shard_map.252.x_ref.dy_ref, ...), custom_call_target="tpu_custom_call" | custom-call | tf_op jit(solution)/shard_map/pallas_call | solution.py:545
  159.9 40.8 %shard_map.254 = (f32[32,2,256]{2,1,0:T(2,128)}, bf16[32,448,128]{2,1,0:T(8,128)(2,1)}, bf16[896,256]{1,0:T(8,128)(2,1)}, f32[448,256]{1,0:T(8,128)}) custom-call(bf16[4,4,2,448,128]{4,3,2,1,0:T(8,128)(2,1)} %bitcast.36, f32[32,2,256]{2,1,0:T(2,128)} %get-tuple-element.35.refs_1_, bf16[448,2560]{1,0:T(8,128)(2,1)} %refs_2_.3, bf16[448,2560]{1,0:T(8,128)(2,1)} %refs_3_.2, ...), custom_call_target="tpu_custom_call" | custom-call | tf_op jit(solution)/shard_map/pallas_call | solution.py:78
  200.7 0.9 broadcast_in_dim.57
  201.6 0.0 copy-done
  201.6 0.7 select_reduce_fusion
  202.3 44.1 %shard_map.255.x_ref.dy_ref = bf16[32,896,256]{2,1,0:T(8,128)(2,1)} custom-call(bf16[896,256]{1,0:T(8,128)(2,1)} %get-tuple-element.37.refs_0_.refs_7_), custom_call_target="tpu_custom_call" | custom-call | tf_op jit(solution)/shard_map/pallas_call | solution.py:78
  246.4 24.1 %shard_map.256 = (f32[2,320,448]{2,1,0:T(8,128)}, f32[2,320,448]{2,1,0:T(8,128)}, f32[2,320,448]{2,1,0:T(8,128)}, bf16[32,448,128]{2,1,0:T(8,128)(2,1)}, f32[32,2,256]{2,1,0:T(2,128)}) custom-call(bf16[32,896,256]{2,1,0:T(8,128)(2,1)} %shard_map.255.x_ref.dy_ref, bf16[32,896,256]{2,1,0:T(8,128)(2,1)} %shard_map.255.x_ref.dy_ref, ...), custom_call_target="tpu_custom_call" | custom-call | tf_op jit(solution)/shard_map/pallas_call | solution.py:545
  270.5 70.7 %shard_map.257 = (f32[32,2,256]{2,1,0:T(2,128)}, bf16[448,256]{1,0:T(8,128)(2,1)}, bf16[448,256]{1,0:T(8,128)(2,1)}) custom-call(bf16[4,4,2,448,128]{4,3,2,1,0:T(8,128)(2,1)} %bitcast.35, bf16[4,4,2,448,128]{4,3,2,1,0:T(8,128)(2,1)} %bitcast.34, f32[32,2,256]{2,1,0:T(2,128)} %get-tuple-element.40.refs_2_, bf16[448,2560]{1,0:T(8,128)(2,1)} %refs_3_.3, ...), custom_call_target="tpu_custom_call" | custom-call | tf_op jit(solution)/shard_map/pallas_call | solution.py:78
  341.2 0.9 broadcast_in_dim.55
  342.1 0.7 select_reduce_fusion.1
  342.8 1.6 copy.30
  344.5 1.6 copy.31
  (7 shorter events, 0.1 us)
Async XLA Ops:
  159.9 41.7 %copy-start = (s32[256,8]{0,1:T(8,128)S(1)}, s32[256,8]{0,1:T(8,128)}, u32[]{:S(2)}) copy-start(s32[256,8]{0,1:T(8,128)} %param.22) | copy-start | bytes 24580
  270.5 71.6 %copy-start.1 = (s32[256,8]{0,1:T(8,128)S(1)}, s32[256,8]{0,1:T(8,128)}, u32[]{:S(2)}) copy-start(s32[256,8]{0,1:T(8,128)} %param.20) | copy-start | bytes 24580
